TPU v7x, 32 devices: a whole 2x2x4 slice. The times are simulated.
32 devices in a mesh: frag: 4 (over x, y), dev: 8 (over z, core).
Axes of the slice: x: 2, y: 2, z: 4, core: 2. Of those that a mesh axis runs over, the one named last changes fastest.
Arguments:
- ao_ints: bfloat16 [256, 64, 64, 64], P(('frag', 'dev')), parts along dimension 0
- coeffs: bfloat16 [256, 64], P('frag'), parts along dimension 0
Outputs:
- output: float32 [256, 64, 4096], P('frag', None, 'dev'), parts along dimension 0
There are 4 independent parts. A program takes and returns all parts, laid end to end along the dimension named above; each array names one.
All inputs are finite; a program needn't handle non-finite values.
Results may differ from a plain program's by a relative error of at most 0.001.
Values are sent between devices in bfloat16 or wider.
A program may use at most 1 GiB of HBM per device.

v0:
```python
import functools

import jax
import jax.numpy as jnp
from jax import lax
from jax.experimental import pallas as pl
from jax.experimental.pallas import tpu as pltpu
from jax.sharding import PartitionSpec as P


N = 64
DEV = 8
ROWS = N // DEV
COLS = N * N // DEV
CHUNKS = COLS // 128
EARLY = ((0, 1), (1, 1), (2, 2), (4, 4))
LATER = ((0, 4), (4, 4))
WHOLE = ((0, 8),)
BF16 = jnp.bfloat16
F32 = jnp.float32


def iota(shape, dim):
    return lax.broadcasted_iota(jnp.int32, shape, dim)


def exchange_kernel(a_hbm, c_hbm, g_ref, l4_ref, l4n_ref, ct_ref, *refs):
    near_refs = refs[:2 * CHUNKS]
    a_vm, c_vm, l_vm, b4_vm, ct_vm, send, recv, a_sem, c_sem, send_sem, recv_sem = refs[2 * CHUNKS:]
    me = lax.axis_index("dev")
    chip = me // 2
    core = me % 2

    load_c = pltpu.make_async_copy(c_hbm, c_vm, c_sem)
    load_c.start()

    def load_row(p):
        return pltpu.make_async_copy(a_hbm.at[p], a_vm.at[p], a_sem.at[p])

    def load_half(h):
        half = pl.ds(32 * h, 32)
        return pltpu.make_async_copy(a_hbm.at[0, half], a_vm.at[0, half], a_sem.at[ROWS * h])

    for h in range(2):
        load_half(h).start()

    barrier = pltpu.get_barrier_semaphore()
    for k in range(1, DEV):
        pl.semaphore_signal(barrier, inc=1, device_id={"dev": (me + k) % DEV}, device_id_type=pl.DeviceIdType.MESH)

    load_c.wait()
    c = c_vm[...]
    nt = (((1,), (1,)), ((), ()))
    wide = (8 * N, 8 * N)

    def kron_rows(first_m, count):
        spread = (iota((8 * count, N), 0) // 8 + first_m == iota((8 * count, N), 1)).astype(BF16)
        rows = lax.dot_general(spread, c, nt, preferred_element_type=F32)
        pair = jnp.concatenate([rows, rows], axis=1)
        tiled = jnp.concatenate([pair] * 4, axis=1)
        shape = (8 * count, 8 * N)
        return jnp.where(iota(shape, 0) % 8 == iota(shape, 1) // N, tiled, 0.0).astype(BF16)

    cf = c.astype(F32)
    cpair = jnp.concatenate([cf, cf], axis=1)
    c4 = jnp.concatenate([cpair, cpair], axis=1)
    c44 = jnp.concatenate([c4] * 4, axis=0)
    quad = (4 * N, 4 * N)
    b4_vm[...] = jnp.where(iota(quad, 0) // N == iota(quad, 1) // N, c44, 0.0).astype(BF16)

    def group(rows, dest, src):
        part = pl.ds(*rows)
        return pltpu.make_async_remote_copy(
            src_ref=send.at[dest, part],
            dst_ref=recv.at[src, part],
            send_sem=send_sem.at[dest, rows[0]],
            recv_sem=recv_sem.at[src, rows[0]],
            device_id={"dev": dest},
            device_id_type=pl.DeviceIdType.MESH,
        )

    def start(rows, to):
        for k in range(2):
            group(rows, 2 * to + k, me).start()

    def sent(groups, to):
        for rows in groups:
            for k in range(2):
                group(rows, 2 * to + k, me).wait_send()

    low = iota((32, 8, 128), 2) < N

    def pieces(p, h, lhs, count, put):
        a = a_vm[p, pl.ds(32 * h, 32)].reshape(4, 8 * N, N)
        left = jnp.concatenate([a[0], a[1]], axis=1)
        right = jnp.concatenate([a[2], a[3]], axis=1)
        a4 = jnp.concatenate([left, right], axis=1)
        t_one = jnp.dot(lhs, a4, preferred_element_type=F32).astype(BF16)
        half = jnp.dot(t_one, b4_vm[...], preferred_element_type=F32)
        pairs = half.reshape(count, 2, 8, 256)
        for t in range(2):
            even = pairs[:, 0, :, 128 * t:128 * t + 128]
            odd = pairs[:, 1, :, 128 * t:128 * t + 128]
            first_rows = jnp.where(low[:count], even, pltpu.roll(odd, N, 2))
            second_rows = jnp.where(low[:count], pltpu.roll(even, N, 2), odd)
            both = jnp.concatenate([first_rows, second_rows], axis=1).astype(BF16)
            for jp in range(count):
                put(jp // 4, pl.ds(32 * h + 16 * t, 16), pl.ds(128 * (jp % 4), 128), both[jp])

    def half_row(p, h):
        def put(dest, q, columns, value):
            send[dest, p, q, columns] = value

        pieces(p, h, l_vm[...], 32, put)

    def chip_piece(to, lhs):
        def put(dest, q, columns, value):
            send[2 * to + dest, 0, q, columns] = value

        for h in range(2):
            pieces(0, h, lhs, 8, put)

    is_edge = jnp.logical_or(chip == 0, chip == 3)
    inward = jnp.where(chip < 2, 1, -1)
    partner = 2 * chip + 1 - core
    near = chip + inward
    far = chip + 2 * inward
    last = chip + 3 * inward
    outward = chip - inward
    beside = jnp.where(is_edge, near, outward)

    first_chip = jnp.where(is_edge, near, far)
    l_vm[:128, :] = kron_rows(16 * first_chip, 16)
    for h in range(2):
        load_half(h).wait()
    for later in range(1, ROWS):
        load_row(later).start()
    chip_piece(first_chip, l_vm[:128, :])
    pl.semaphore_wait(barrier, DEV - 1)
    start(EARLY[0], first_chip)

    l_vm[...] = kron_rows(0, N)

    def l_rows(to):
        return l_vm[pl.ds(pl.multiple_of(128 * to, 128), 128), :]

    second_chip = jnp.where(is_edge, far, outward)
    chip_piece(second_chip, l_rows(second_chip))

    @pl.when(jnp.logical_not(is_edge))
    def _():
        start(EARLY[0], outward)

    fourth_chip = jnp.where(is_edge, last, near)
    chip_piece(fourth_chip, l_rows(fourth_chip))
    chip_piece(chip, l_rows(chip))
    group(EARLY[0], partner, me).start()

    def make_row(p, carry):
        load_row(p).wait()
        for h in range(2):
            half_row(p, h)
        for rows in EARLY[1:]:
            @pl.when(p == sum(rows) - 1)
            def _():
                start(rows, beside)

                @pl.when(jnp.logical_not(is_edge))
                def _():
                    start(rows, far)

                group(rows, partner, me).start()

        return carry

    lax.fori_loop(1, ROWS, make_row, 0)

    @pl.when(is_edge)
    def _():
        for rows in LATER:
            start(rows, far)
        for rows in WHOLE:
            start(rows, last)

    for side, dest in ((0, 2 * near + core), (1, 2 * near + 1 - core)):
        for chunk in range(CHUNKS):
            near_refs[side * CHUNKS + chunk][...] = send[dest, :, :, pl.ds(128 * chunk, 128)]

    c = c_vm[...]
    spread = (iota((8 * N, N), 0) // 8 == iota((8 * N, N), 1)).astype(BF16)
    rows = lax.dot_general(spread, c, nt, preferred_element_type=F32)
    widen = (iota((N, 8 * N), 0) == iota((N, 8 * N), 1) // 8).astype(BF16)
    full = jnp.dot(rows.astype(BF16), widen, preferred_element_type=F32)
    l4_ref[...] = jnp.where(iota(wide, 0) % 8 == iota(wide, 1) % 8, full, 0.0).astype(BF16)
    l4n_ref[...] = l4_ref[:, pl.ds(pl.multiple_of(128 * near, 128), 128)]
    eye = (iota((N, N), 0) == iota((N, N), 1)).astype(BF16)
    ct_vm[...] = lax.dot_general(eye, c, nt, preferred_element_type=F32).astype(BF16)
    ct_ref[...] = ct_vm[...]

    def third(src, p, first, second):
        g0 = jnp.dot(ct_vm[...], first, preferred_element_type=F32).reshape(8, 8, COLS)
        g1 = jnp.dot(ct_vm[...], second, preferred_element_type=F32).reshape(8, 8, COLS)
        at = pl.multiple_of(N * src + 8 * p, 16)
        g_ref[:, pl.ds(at, 16), :] = jnp.concatenate([g0, g1], axis=1).astype(BF16)

    def own(t, carry):
        third(me, 2 * t, send[me, 2 * t], send[me, 2 * t + 1])
        return carry

    lax.fori_loop(0, ROWS // 2, own, 0)

    def take(groups, sources):
        for rows in groups:
            for src in sources:
                group(rows, src, src).wait_recv()
            if sum(rows) % 2 == 0:
                begin = rows[0] // 2 * 2

                def body(t, carry):
                    for src in sources:
                        p = begin + 2 * t
                        third(src, p, recv[src, p], recv[src, p + 1])
                    return carry

                lax.fori_loop(0, (sum(rows) - begin) // 2, body, 0)

    take(EARLY, [partner])

    @pl.when(jnp.logical_not(is_edge))
    def _():
        g_ref[:, pl.ds(pl.multiple_of(2 * N * near, 16), 2 * N), :] = jnp.zeros((8, 2 * N, COLS), BF16)

    take(EARLY, [2 * beside, 2 * beside + 1])

    for rows in EARLY:
        group(rows, partner, me).wait_send()
    sent(EARLY, beside)

    @pl.when(is_edge)
    def _():
        take(EARLY, [2 * far, 2 * far + 1])
        take(WHOLE, [2 * last, 2 * last + 1])
        sent(LATER, far)
        sent(WHOLE, last)

    @pl.when(jnp.logical_not(is_edge))
    def _():
        take(LATER, [2 * far, 2 * far + 1])
        sent(EARLY, far)


def most_kernel(g_ref, l4_ref, v_ref):
    for ag in range(8):
        v_ref[ag] = jnp.dot(l4_ref[...], g_ref[ag], preferred_element_type=F32)


def chunk_kernel(chunk, same_ref, other_ref, ct_ref, l4n_ref, most_ref, *refs):
    v_hbm, g_vm, v_vm, v_sem = refs[-4:]
    core = lax.axis_index("dev") % 2
    for side, ref in ((core, same_ref), (1 - core, other_ref)):
        for p in range(0, ROWS, 2):
            g0 = jnp.dot(ct_ref[...], ref[p], preferred_element_type=F32).reshape(8, 8, 128)
            g1 = jnp.dot(ct_ref[...], ref[p + 1], preferred_element_type=F32).reshape(8, 8, 128)
            at = pl.multiple_of(N * side + 8 * p, 16)
            g_vm[:, pl.ds(at, 16), :] = jnp.concatenate([g0, g1], axis=1).astype(BF16)

    def put(ag):
        return pltpu.make_async_copy(v_vm.at[ag], v_hbm.at[:, pl.ds(8 * ag, 8), pl.ds(128 * chunk, 128)], v_sem.at[ag])

    for ag in range(8):
        part = jnp.dot(l4n_ref[...], g_vm[ag], preferred_element_type=F32)
        v_vm[ag] = (part + most_ref[ag, :, 128 * chunk:128 * chunk + 128]).reshape(N, 8, 128)
        put(ag).start()
    for ag in range(8):
        put(ag).wait()


def solution(mesh):
    def local_transform(ao_rows, coeffs):
        vmem = pl.BlockSpec(memory_space=pltpu.VMEM)
        anywhere = pl.BlockSpec(memory_space=pltpu.HBM)
        sds = jax.ShapeDtypeStruct
        outs = (
            sds((8, 8 * N, COLS), BF16),
            sds((8 * N, 8 * N), BF16),
            sds((8 * N, 2 * N), BF16),
            sds((N, N), BF16),
        ) + (sds((ROWS, N, 128), BF16),) * (2 * CHUNKS)
        g, l4, l4n, ct, *near = pl.pallas_call(
            exchange_kernel,
            out_shape=outs,
            in_specs=[anywhere, anywhere],
            out_specs=(vmem,) * len(outs),
            scratch_shapes=[
                pltpu.VMEM((ROWS, N, N, N), BF16),
                pltpu.VMEM((N, N), BF16),
                pltpu.VMEM((8 * N, 8 * N), BF16),
                pltpu.VMEM((4 * N, 4 * N), BF16),
                pltpu.VMEM((N, N), BF16),
                pltpu.VMEM((DEV, ROWS, N, COLS), BF16),
                pltpu.VMEM((DEV, ROWS, N, COLS), BF16),
                pltpu.SemaphoreType.DMA((ROWS + 1,)),
                pltpu.SemaphoreType.DMA,
                pltpu.SemaphoreType.DMA((DEV, ROWS)),
                pltpu.SemaphoreType.DMA((DEV, ROWS)),
            ],
            compiler_params=pltpu.CompilerParams(collective_id=0, has_side_effects=True, vmem_limit_bytes=40 * 2**20),
            name="exchange",
        )(pltpu.with_memory_space_constraint(ao_rows, pltpu.HBM), pltpu.with_memory_space_constraint(coeffs, pltpu.HBM))
        same = [(2, 4), (3, 5), (4, 2), (5, 3)]
        other = [(2, 5), (3, 4), (4, 3), (5, 2)]
        arrived = []
        for chunk in range(CHUNKS):
            pair = []
            for side, perm in enumerate((same, other)):
                pair.append(lax.ppermute(near[side * CHUNKS + chunk], "dev", perm))
            arrived.append(pair)
        most = pl.pallas_call(
            most_kernel,
            out_shape=sds((8, 8 * N, COLS), F32),
            in_specs=[vmem, vmem],
            out_specs=vmem,
            compiler_params=pltpu.CompilerParams(vmem_limit_bytes=12 * 2**20),
            cost_estimate=pl.CostEstimate(flops=2 * 8 * 512**3, bytes_accessed=12 * 2**20, transcendentals=0),
            name="most",
        )(g, l4)
        v = None
        for chunk in range(CHUNKS):
            operands = (*arrived[chunk], ct, l4n, most) + (() if v is None else (v,))
            v = pl.pallas_call(
                functools.partial(chunk_kernel, chunk),
                out_shape=sds((N, N, COLS), F32),
                in_specs=[vmem] * 5 + ([] if v is None else [anywhere]),
                out_specs=anywhere,
                scratch_shapes=[
                    pltpu.VMEM((8, 2 * N, 128), BF16),
                    pltpu.VMEM((8, N, 8, 128), F32),
                    pltpu.SemaphoreType.DMA((8,)),
                ],
                input_output_aliases={} if v is None else {5: 0},
                compiler_params=pltpu.CompilerParams(vmem_limit_bytes=12 * 2**20),
                cost_estimate=pl.CostEstimate(flops=2 * 8 * 512 * 128 * 128, bytes_accessed=4 * 2**20, transcendentals=0),
            )(*operands)
        return v

    return jax.shard_map(local_transform, mesh=mesh, in_specs=(P(('frag', 'dev')), P('frag')), out_specs=P('frag', None, 'dev'), check_vma=False)
```

profile of v0, /device:TPU:13, one launch (start us, length us, event | category | flops | bytes accessed | tf_op | source)
XLA Modules:
  0.0 100.9 jit_solution(15686696974169615372)
XLA Ops:
  0.0 52.3 %exchange.1 = (bf16[8,512,512]{2,1,0:T(8,128)(2,1)S(1)}, bf16[512,512]{1,0:T(8,128)(2,1)S(1)}, bf16[512,128]{1,0:T(8,128)(2,1)S(1)}, bf16[64,64]{1,0:T(8,128)(2,...) custom-call(bf16[8,64,64,64]{3,2,1,0:T(8,128)(2,1)} %a_hbm.1, ...), custom_call_target="tpu_custom_call" | custom-call | tf_op jit(solution)/shard_map/exchange/pallas_call | solution.py:289
  52.3 2.9 %collective-permute-start.4 = (bf16[8,64,128]{2,1,0:T(8,128)(2,1)S(1)}, bf16[8,64,128]{2,1,0:T(8,128)(2,1)S(1)}, u32[]{:S(2)}, u32[]{:S(2)}) collective-permute-start(bf16[8,64,128]{2,1,0:T(8,128)(2,1)S(1)} %get-tuple-element.25), channel_id=1, source_target_pairs={{2,4},{3,5},{4,2},{5,3},{10,12},{11,13},{12,10},{13,11},{18,20},{1... | collective-permute-start | bytes 393224 | tf_op jit(solution)/shard_map/ppermute | solution.py:316
  55.2 2.3 %collective-permute-start.6 = (bf16[8,64,128]{2,1,0:T(8,128)(2,1)S(1)}, bf16[8,64,128]{2,1,0:T(8,128)(2,1)S(1)}, u32[]{:S(2)}, u32[]{:S(2)}) collective-permute-start(bf16[8,64,128]{2,1,0:T(8,128)(2,1)S(1)} %get-tuple-element.27), channel_id=1, source_target_pairs={{2,4},{3,5},{4,2},{5,3},{10,12},{11,13},{12,10},{13,11},{18,20},{1... | collective-permute-start | bytes 393224 | tf_op jit(solution)/shard_map/ppermute | solution.py:316
  57.6 2.0 %collective-permute-start.7 = (bf16[8,64,128]{2,1,0:T(8,128)(2,1)S(1)}, bf16[8,64,128]{2,1,0:T(8,128)(2,1)S(1)}, u32[]{:S(2)}, u32[]{:S(2)}) collective-permute-start(bf16[8,64,128]{2,1,0:T(8,128)(2,1)S(1)} %get-tuple-element.28), channel_id=1, source_target_pairs={{2,5},{3,4},{4,3},{5,2},{10,13},{11,12},{12,11},{13,10},{18,21},{1... | collective-permute-start | bytes 393224 | tf_op jit(solution)/shard_map/ppermute | solution.py:316
  59.6 2.9 %collective-permute-start = (bf16[8,64,128]{2,1,0:T(8,128)(2,1)S(1)}, bf16[8,64,128]{2,1,0:T(8,128)(2,1)S(1)}, u32[]{:S(2)}, u32[]{:S(2)}) collective-permute-start(bf16[8,64,128]{2,1,0:T(8,128)(2,1)S(1)} %get-tuple-element.17), channel_id=1, source_target_pairs={{2,4},{3,5},{4,2},{5,3},{10,12},{11,13},{12,10},{13,11},{18,20},{1... | collective-permute-start | bytes 393224 | tf_op jit(solution)/shard_map/ppermute | solution.py:316
  62.4 3.9 %collective-permute-start.1 = (bf16[8,64,128]{2,1,0:T(8,128)(2,1)S(1)}, bf16[8,64,128]{2,1,0:T(8,128)(2,1)S(1)}, u32[]{:S(2)}, u32[]{:S(2)}) collective-permute-start(bf16[8,64,128]{2,1,0:T(8,128)(2,1)S(1)} %get-tuple-element.18), channel_id=1, source_target_pairs={{2,5},{3,4},{4,3},{5,2},{10,13},{11,12},{12,11},{13,10},{18,21},{1... | collective-permute-start | bytes 393224 | tf_op jit(solution)/shard_map/ppermute | solution.py:316
  66.4 9.4 %collective-permute-done.4.same_ref = bf16[8,64,128]{2,1,0:T(8,128)(2,1)S(1)} collective-permute-done((bf16[8,64,128]{2,1,0:T(8,128)(2,1)S(1)}, bf16[8,64,128]{2,1,0:T(8,128)(2,1)S(1)}, u32[]{:S(2)}, u32[]{:S(2)}) %collective-permute-start.4) | collective-permute-done | bytes 131104 | tf_op jit(solution)/shard_map/ppermute | solution.py:316
  75.8 2.9 %collective-permute-start.2 = (bf16[8,64,128]{2,1,0:T(8,128)(2,1)S(1)}, bf16[8,64,128]{2,1,0:T(8,128)(2,1)S(1)}, u32[]{:S(2)}, u32[]{:S(2)}) collective-permute-start(bf16[8,64,128]{2,1,0:T(8,128)(2,1)S(1)} %get-tuple-element.23), channel_id=1, source_target_pairs={{2,4},{3,5},{4,2},{5,3},{10,12},{11,13},{12,10},{13,11},{18,20},{1... | collective-permute-start | bytes 393224 | tf_op jit(solution)/shard_map/ppermute | solution.py:316
  78.8 0.0 collective-permute-done.6.same_ref
  78.8 2.9 %collective-permute-start.3 = (bf16[8,64,128]{2,1,0:T(8,128)(2,1)S(1)}, bf16[8,64,128]{2,1,0:T(8,128)(2,1)S(1)}, u32[]{:S(2)}, u32[]{:S(2)}) collective-permute-start(bf16[8,64,128]{2,1,0:T(8,128)(2,1)S(1)} %get-tuple-element.24), channel_id=1, source_target_pairs={{2,5},{3,4},{4,3},{5,2},{10,13},{11,12},{12,11},{13,10},{18,21},{1... | collective-permute-start | bytes 393224 | tf_op jit(solution)/shard_map/ppermute | solution.py:316
  81.7 0.0 collective-permute-done.7.other_ref
  81.7 3.0 %collective-permute-start.5 = (bf16[8,64,128]{2,1,0:T(8,128)(2,1)S(1)}, bf16[8,64,128]{2,1,0:T(8,128)(2,1)S(1)}, u32[]{:S(2)}, u32[]{:S(2)}) collective-permute-start(bf16[8,64,128]{2,1,0:T(8,128)(2,1)S(1)} %get-tuple-element.26), channel_id=1, source_target_pairs={{2,5},{3,4},{4,3},{5,2},{10,13},{11,12},{12,11},{13,10},{18,21},{1... | collective-permute-start | bytes 393224 | tf_op jit(solution)/shard_map/ppermute | solution.py:316
  84.7 2.3 %most.1.most_ref = f32[8,512,512]{2,1,0:T(8,128)S(1)} custom-call(bf16[8,512,512]{2,1,0:T(8,128)(2,1)S(1)} %get-tuple-element.21.g_ref, bf16[512,512]{1,0:T(8,128)(2,1)S(1)} %get-tuple-element.22.l4_ref), custom_call_target="tpu_custom_call" | custom-call | flops 2147483648 | bytes 12582912 | tf_op jit(solution)/shard_map/most/pallas_call | solution.py:318
  87.0 1.8 %shard_map.28.refs_0_ = f32[64,64,512]{2,1,0:T(8,128)} custom-call(bf16[8,64,128]{2,1,0:T(8,128)(2,1)S(1)} %collective-permute-done.6.same_ref, bf16[8,64,128]{2,1,0:T(8,128)(2,1)S(1)} %collective-permute-done.7.other_ref, bf16[64,64]{1,0:T(8,128)(2,1)S(1)} %get-tuple-element.19.ct_ref, bf16[512,128]{1,0:T(8,128)(2,1)S(1)} %get-tuple-element.20.l4n_ref, ...), custom_call_target="tpu_custom_call" | custom-call | flops 134217728 | bytes 4194304 | tf_op jit(solution)/shard_map/pallas_call | solution.py:330
  88.9 6.5 %collective-permute-done.5.other_ref = bf16[8,64,128]{2,1,0:T(8,128)(2,1)S(1)} collective-permute-done((bf16[8,64,128]{2,1,0:T(8,128)(2,1)S(1)}, bf16[8,64,128]{2,1,0:T(8,128)(2,1)S(1)}, u32[]{:S(2)}, u32[]{:S(2)}) %collective-permute-start.5) | collective-permute-done | bytes 131104 | tf_op jit(solution)/shard_map/ppermute | solution.py:316
  95.3 1.8 %shard_map.29.refs_0_ = f32[64,64,512]{2,1,0:T(8,128)} custom-call(bf16[8,64,128]{2,1,0:T(8,128)(2,1)S(1)} %collective-permute-done.4.same_ref, bf16[8,64,128]{2,1,0:T(8,128)(2,1)S(1)} %collective-permute-done.5.other_ref, bf16[64,64]{1,0:T(8,128)(2,1)S(1)} %get-tuple-element.19.ct_ref, ...), custom_call_target="tpu_custom_call", output_to_operand_aliasing={{}: (5, {})} | custom-call | flops 134217728 | bytes 4194304 | tf_op jit(solution)/shard_map/pallas_call | solution.py:330
  97.2 0.0 collective-permute-done.2.same_ref
  97.2 0.0 collective-permute-done.3.other_ref
  97.2 1.8 %shard_map.30.refs_0_ = f32[64,64,512]{2,1,0:T(8,128)} custom-call(bf16[8,64,128]{2,1,0:T(8,128)(2,1)S(1)} %collective-permute-done.2.same_ref, bf16[8,64,128]{2,1,0:T(8,128)(2,1)S(1)} %collective-permute-done.3.other_ref, bf16[64,64]{1,0:T(8,128)(2,1)S(1)} %get-tuple-element.19.ct_ref, ...), custom_call_target="tpu_custom_call", output_to_operand_aliasing={{}: (5, {})} | custom-call | flops 134217728 | bytes 4194304 | tf_op jit(solution)/shard_map/pallas_call | solution.py:330
  99.0 0.0 collective-permute-done.same_ref
  99.0 0.0 collective-permute-done.1.other_ref
  99.0 1.8 %shard_map.31 = f32[64,64,512]{2,1,0:T(8,128)} custom-call(bf16[8,64,128]{2,1,0:T(8,128)(2,1)S(1)} %collective-permute-done.same_ref, bf16[8,64,128]{2,1,0:T(8,128)(2,1)S(1)} %collective-permute-done.1.other_ref, bf16[64,64]{1,0:T(8,128)(2,1)S(1)} %get-tuple-element.19.ct_ref, ...), custom_call_target="tpu_custom_call", output_to_operand_aliasing={{}: (5, {})} | custom-call | flops 134217728 | bytes 4194304 | tf_op jit(solution)/shard_map/pallas_call | solution.py:330
Async XLA Ops:
  52.3 23.6 %collective-permute-start.4 = (bf16[8,64,128]{2,1,0:T(8,128)(2,1)S(1)}, bf16[8,64,128]{2,1,0:T(8,128)(2,1)S(1)}, u32[]{:S(2)}, u32[]{:S(2)}) collective-permute-start(bf16[8,64,128]{2,1,0:T(8,128)(2,1)S(1)} %get-tuple-element.25), channel_id=1, source_target_pairs={{2,4},{3,5},{4,2},{5,3},{10,12},{11,13},{12,10},{13,11},{18,20},{1... | collective-permute-start | bytes 393224 | tf_op jit(solution)/shard_map/ppermute | solution.py:316
  55.2 23.5 %collective-permute-start.6 = (bf16[8,64,128]{2,1,0:T(8,128)(2,1)S(1)}, bf16[8,64,128]{2,1,0:T(8,128)(2,1)S(1)}, u32[]{:S(2)}, u32[]{:S(2)}) collective-permute-start(bf16[8,64,128]{2,1,0:T(8,128)(2,1)S(1)} %get-tuple-element.27), channel_id=1, source_target_pairs={{2,4},{3,5},{4,2},{5,3},{10,12},{11,13},{12,10},{13,11},{18,20},{1... | collective-permute-start | bytes 393224 | tf_op jit(solution)/shard_map/ppermute | solution.py:316
  57.6 24.1 %collective-permute-start.7 = (bf16[8,64,128]{2,1,0:T(8,128)(2,1)S(1)}, bf16[8,64,128]{2,1,0:T(8,128)(2,1)S(1)}, u32[]{:S(2)}, u32[]{:S(2)}) collective-permute-start(bf16[8,64,128]{2,1,0:T(8,128)(2,1)S(1)} %get-tuple-element.28), channel_id=1, source_target_pairs={{2,5},{3,4},{4,3},{5,2},{10,13},{11,12},{12,11},{13,10},{18,21},{1... | collective-permute-start | bytes 393224 | tf_op jit(solution)/shard_map/ppermute | solution.py:316
  59.6 39.5 %collective-permute-start = (bf16[8,64,128]{2,1,0:T(8,128)(2,1)S(1)}, bf16[8,64,128]{2,1,0:T(8,128)(2,1)S(1)}, u32[]{:S(2)}, u32[]{:S(2)}) collective-permute-start(bf16[8,64,128]{2,1,0:T(8,128)(2,1)S(1)} %get-tuple-element.17), channel_id=1, source_target_pairs={{2,4},{3,5},{4,2},{5,3},{10,12},{11,13},{12,10},{13,11},{18,20},{1... | collective-permute-start | bytes 393224 | tf_op jit(solution)/shard_map/ppermute | solution.py:316
  62.4 36.6 %collective-permute-start.1 = (bf16[8,64,128]{2,1,0:T(8,128)(2,1)S(1)}, bf16[8,64,128]{2,1,0:T(8,128)(2,1)S(1)}, u32[]{:S(2)}, u32[]{:S(2)}) collective-permute-start(bf16[8,64,128]{2,1,0:T(8,128)(2,1)S(1)} %get-tuple-element.18), channel_id=1, source_target_pairs={{2,5},{3,4},{4,3},{5,2},{10,13},{11,12},{12,11},{13,10},{18,21},{1... | collective-permute-start | bytes 393224 | tf_op jit(solution)/shard_map/ppermute | solution.py:316
  75.8 21.3 %collective-permute-start.2 = (bf16[8,64,128]{2,1,0:T(8,128)(2,1)S(1)}, bf16[8,64,128]{2,1,0:T(8,128)(2,1)S(1)}, u32[]{:S(2)}, u32[]{:S(2)}) collective-permute-start(bf16[8,64,128]{2,1,0:T(8,128)(2,1)S(1)} %get-tuple-element.23), channel_id=1, source_target_pairs={{2,4},{3,5},{4,2},{5,3},{10,12},{11,13},{12,10},{13,11},{18,20},{1... | collective-permute-start | bytes 393224 | tf_op jit(solution)/shard_map/ppermute | solution.py:316
  78.8 18.4 %collective-permute-start.3 = (bf16[8,64,128]{2,1,0:T(8,128)(2,1)S(1)}, bf16[8,64,128]{2,1,0:T(8,128)(2,1)S(1)}, u32[]{:S(2)}, u32[]{:S(2)}) collective-permute-start(bf16[8,64,128]{2,1,0:T(8,128)(2,1)S(1)} %get-tuple-element.24), channel_id=1, source_target_pairs={{2,5},{3,4},{4,3},{5,2},{10,13},{11,12},{12,11},{13,10},{18,21},{1... | collective-permute-start | bytes 393224 | tf_op jit(solution)/shard_map/ppermute | solution.py:316
  81.7 13.6 %collective-permute-start.5 = (bf16[8,64,128]{2,1,0:T(8,128)(2,1)S(1)}, bf16[8,64,128]{2,1,0:T(8,128)(2,1)S(1)}, u32[]{:S(2)}, u32[]{:S(2)}) collective-permute-start(bf16[8,64,128]{2,1,0:T(8,128)(2,1)S(1)} %get-tuple-element.26), channel_id=1, source_target_pairs={{2,5},{3,4},{4,3},{5,2},{10,13},{11,12},{12,11},{13,10},{18,21},{1... | collective-permute-start | bytes 393224 | tf_op jit(solution)/shard_map/ppermute | solution.py:316
where the time goes:
time: 101 us
  Pallas kernels  61.9 us (61%)
  starting transfers between devices  22.9 us (23%)
  waiting for transfers between devices  15.9 us (16%)
    pallas_call x1, Pallas kernels, local_transform(): pl.pallas_call(exchange_kernel, out_shape=outs, in_specs=[anywhere, anywh...  52.3 us
    ppermute x8, starting transfers between devices, local_transform(): pair.append(lax.ppermute(near[side * CHUNKS + chunk], 'dev', perm))  22.9 us
    ppermute x8, waiting for transfers between devices, local_transform(): pair.append(lax.ppermute(near[side * CHUNKS + chunk], 'dev', perm))  15.9 us
    pallas_call x4, Pallas kernels, local_transform(): pl.pallas_call(functools.partial(chunk_kernel, chunk), out_shape=sds((N,...  7.34 us
    pallas_call x1, Pallas kernels, local_transform(): pl.pallas_call(most_kernel, out_shape=sds((8, 8 * N, COLS), F32), in_spec...  2.34 us
  transfers between devices with their start and end apart: 8, of which 2 were waited for; matrix products, arithmetic and copies ran while one was open for 0% of the time, Pallas kernels for 8%

commit v1 on v0

--- a/solution.py
+++ b/solution.py
@@ -133,7 +133,7 @@
     l_vm[:128, :] = kron_rows(16 * first_chip, 16)
     for h in range(2):
         load_half(h).wait()
-    for later in range(1, ROWS):
+    for later in (1, 2):
         load_row(later).start()
     chip_piece(first_chip, l_vm[:128, :])
     pl.semaphore_wait(barrier, DEV - 1)
@@ -158,6 +158,11 @@
 
     def make_row(p, carry):
         load_row(p).wait()
+
+        @pl.when(p < ROWS - 2)
+        def _():
+            load_row(p + 2).start()
+
         for h in range(2):
             half_row(p, h)
         for rows in EARLY[1:]:

time: 101 us -> 101 us (level)
  the two profiles are of different devices: /device:TPU:13 before, /device:TPU:15 now
where the time goes in v1:
time: 101 us
  Pallas kernels  61.9 us (61%)
  starting transfers between devices  22.9 us (23%)
  waiting for transfers between devices  15.9 us (16%)
    pallas_call x1, Pallas kernels, local_transform(): pl.pallas_call(exchange_kernel, out_shape=outs, in_specs=[anywhere, anywh...  52.3 us
    ppermute x8, starting transfers between devices, local_transform(): pair.append(lax.ppermute(near[side * CHUNKS + chunk], 'dev', perm))  22.9 us
    ppermute x8, waiting for transfers between devices, local_transform(): pair.append(lax.ppermute(near[side * CHUNKS + chunk], 'dev', perm))  15.9 us
    pallas_call x4, Pallas kernels, local_transform(): pl.pallas_call(functools.partial(chunk_kernel, chunk), out_shape=sds((N,...  7.34 us
    pallas_call x1, Pallas kernels, local_transform(): pl.pallas_call(most_kernel, out_shape=sds((8, 8 * N, COLS), F32), in_spec...  2.34 us
  transfers between devices with their start and end apart: 8, of which 2 were waited for; matrix products, arithmetic and copies ran while one was open for 0% of the time, Pallas kernels for 8%

profile of v1, /device:TPU:15, one launch (start us, length us, event | category | flops | bytes accessed | tf_op | source)
XLA Modules:
  0.0 100.9 jit_solution(10418448831997636754)
XLA Ops:
  0.0 52.3 %exchange.1 = (bf16[8,512,512]{2,1,0:T(8,128)(2,1)S(1)}, bf16[512,512]{1,0:T(8,128)(2,1)S(1)}, bf16[512,128]{1,0:T(8,128)(2,1)S(1)}, bf16[64,64]{1,0:T(8,128)(2,...) custom-call(bf16[8,64,64,64]{3,2,1,0:T(8,128)(2,1)} %a_hbm.1, ...), custom_call_target="tpu_custom_call" | custom-call | tf_op jit(solution)/shard_map/exchange/pallas_call | solution.py:294
  52.3 2.9 %collective-permute-start.4 = (bf16[8,64,128]{2,1,0:T(8,128)(2,1)S(1)}, bf16[8,64,128]{2,1,0:T(8,128)(2,1)S(1)}, u32[]{:S(2)}, u32[]{:S(2)}) collective-permute-start(bf16[8,64,128]{2,1,0:T(8,128)(2,1)S(1)} %get-tuple-element.25), channel_id=1, source_target_pairs={{2,4},{3,5},{4,2},{5,3},{10,12},{11,13},{12,10},{13,11},{18,20},{1... | collective-permute-start | bytes 393224 | tf_op jit(solution)/shard_map/ppermute | solution.py:321
  55.2 2.4 %collective-permute-start.6 = (bf16[8,64,128]{2,1,0:T(8,128)(2,1)S(1)}, bf16[8,64,128]{2,1,0:T(8,128)(2,1)S(1)}, u32[]{:S(2)}, u32[]{:S(2)}) collective-permute-start(bf16[8,64,128]{2,1,0:T(8,128)(2,1)S(1)} %get-tuple-element.27), channel_id=1, source_target_pairs={{2,4},{3,5},{4,2},{5,3},{10,12},{11,13},{12,10},{13,11},{18,20},{1... | collective-permute-start | bytes 393224 | tf_op jit(solution)/shard_map/ppermute | solution.py:321
  57.6 2.0 %collective-permute-start.7 = (bf16[8,64,128]{2,1,0:T(8,128)(2,1)S(1)}, bf16[8,64,128]{2,1,0:T(8,128)(2,1)S(1)}, u32[]{:S(2)}, u32[]{:S(2)}) collective-permute-start(bf16[8,64,128]{2,1,0:T(8,128)(2,1)S(1)} %get-tuple-element.28), channel_id=1, source_target_pairs={{2,5},{3,4},{4,3},{5,2},{10,13},{11,12},{12,11},{13,10},{18,21},{1... | collective-permute-start | bytes 393224 | tf_op jit(solution)/shard_map/ppermute | solution.py:321
  59.5 2.9 %collective-permute-start = (bf16[8,64,128]{2,1,0:T(8,128)(2,1)S(1)}, bf16[8,64,128]{2,1,0:T(8,128)(2,1)S(1)}, u32[]{:S(2)}, u32[]{:S(2)}) collective-permute-start(bf16[8,64,128]{2,1,0:T(8,128)(2,1)S(1)} %get-tuple-element.17), channel_id=1, source_target_pairs={{2,4},{3,5},{4,2},{5,3},{10,12},{11,13},{12,10},{13,11},{18,20},{1... | collective-permute-start | bytes 393224 | tf_op jit(solution)/shard_map/ppermute | solution.py:321
  62.4 3.9 %collective-permute-start.1 = (bf16[8,64,128]{2,1,0:T(8,128)(2,1)S(1)}, bf16[8,64,128]{2,1,0:T(8,128)(2,1)S(1)}, u32[]{:S(2)}, u32[]{:S(2)}) collective-permute-start(bf16[8,64,128]{2,1,0:T(8,128)(2,1)S(1)} %get-tuple-element.18), channel_id=1, source_target_pairs={{2,5},{3,4},{4,3},{5,2},{10,13},{11,12},{12,11},{13,10},{18,21},{1... | collective-permute-start | bytes 393224 | tf_op jit(solution)/shard_map/ppermute | solution.py:321
  66.4 9.5 %collective-permute-done.4.same_ref = bf16[8,64,128]{2,1,0:T(8,128)(2,1)S(1)} collective-permute-done((bf16[8,64,128]{2,1,0:T(8,128)(2,1)S(1)}, bf16[8,64,128]{2,1,0:T(8,128)(2,1)S(1)}, u32[]{:S(2)}, u32[]{:S(2)}) %collective-permute-start.4) | collective-permute-done | bytes 131104 | tf_op jit(solution)/shard_map/ppermute | solution.py:321
  75.8 2.9 %collective-permute-start.2 = (bf16[8,64,128]{2,1,0:T(8,128)(2,1)S(1)}, bf16[8,64,128]{2,1,0:T(8,128)(2,1)S(1)}, u32[]{:S(2)}, u32[]{:S(2)}) collective-permute-start(bf16[8,64,128]{2,1,0:T(8,128)(2,1)S(1)} %get-tuple-element.23), channel_id=1, source_target_pairs={{2,4},{3,5},{4,2},{5,3},{10,12},{11,13},{12,10},{13,11},{18,20},{1... | collective-permute-start | bytes 393224 | tf_op jit(solution)/shard_map/ppermute | solution.py:321
  78.8 0.0 collective-permute-done.6.same_ref
  78.8 2.9 %collective-permute-start.3 = (bf16[8,64,128]{2,1,0:T(8,128)(2,1)S(1)}, bf16[8,64,128]{2,1,0:T(8,128)(2,1)S(1)}, u32[]{:S(2)}, u32[]{:S(2)}) collective-permute-start(bf16[8,64,128]{2,1,0:T(8,128)(2,1)S(1)} %get-tuple-element.24), channel_id=1, source_target_pairs={{2,5},{3,4},{4,3},{5,2},{10,13},{11,12},{12,11},{13,10},{18,21},{1... | collective-permute-start | bytes 393224 | tf_op jit(solution)/shard_map/ppermute | solution.py:321
  81.7 0.0 collective-permute-done.7.other_ref
  81.7 3.0 %collective-permute-start.5 = (bf16[8,64,128]{2,1,0:T(8,128)(2,1)S(1)}, bf16[8,64,128]{2,1,0:T(8,128)(2,1)S(1)}, u32[]{:S(2)}, u32[]{:S(2)}) collective-permute-start(bf16[8,64,128]{2,1,0:T(8,128)(2,1)S(1)} %get-tuple-element.26), channel_id=1, source_target_pairs={{2,5},{3,4},{4,3},{5,2},{10,13},{11,12},{12,11},{13,10},{18,21},{1... | collective-permute-start | bytes 393224 | tf_op jit(solution)/shard_map/ppermute | solution.py:321
  84.7 2.3 %most.1.most_ref = f32[8,512,512]{2,1,0:T(8,128)S(1)} custom-call(bf16[8,512,512]{2,1,0:T(8,128)(2,1)S(1)} %get-tuple-element.21.g_ref, bf16[512,512]{1,0:T(8,128)(2,1)S(1)} %get-tuple-element.22.l4_ref), custom_call_target="tpu_custom_call" | custom-call | flops 2147483648 | bytes 12582912 | tf_op jit(solution)/shard_map/most/pallas_call | solution.py:323
  87.0 1.8 %shard_map.28.refs_0_ = f32[64,64,512]{2,1,0:T(8,128)} custom-call(bf16[8,64,128]{2,1,0:T(8,128)(2,1)S(1)} %collective-permute-done.6.same_ref, bf16[8,64,128]{2,1,0:T(8,128)(2,1)S(1)} %collective-permute-done.7.other_ref, bf16[64,64]{1,0:T(8,128)(2,1)S(1)} %get-tuple-element.19.ct_ref, bf16[512,128]{1,0:T(8,128)(2,1)S(1)} %get-tuple-element.20.l4n_ref, ...), custom_call_target="tpu_custom_call" | custom-call | flops 134217728 | bytes 4194304 | tf_op jit(solution)/shard_map/pallas_call | solution.py:335
  88.9 6.5 %collective-permute-done.5.other_ref = bf16[8,64,128]{2,1,0:T(8,128)(2,1)S(1)} collective-permute-done((bf16[8,64,128]{2,1,0:T(8,128)(2,1)S(1)}, bf16[8,64,128]{2,1,0:T(8,128)(2,1)S(1)}, u32[]{:S(2)}, u32[]{:S(2)}) %collective-permute-start.5) | collective-permute-done | bytes 131104 | tf_op jit(solution)/shard_map/ppermute | solution.py:321
  95.3 1.8 %shard_map.29.refs_0_ = f32[64,64,512]{2,1,0:T(8,128)} custom-call(bf16[8,64,128]{2,1,0:T(8,128)(2,1)S(1)} %collective-permute-done.4.same_ref, bf16[8,64,128]{2,1,0:T(8,128)(2,1)S(1)} %collective-permute-done.5.other_ref, bf16[64,64]{1,0:T(8,128)(2,1)S(1)} %get-tuple-element.19.ct_ref, ...), custom_call_target="tpu_custom_call", output_to_operand_aliasing={{}: (5, {})} | custom-call | flops 134217728 | bytes 4194304 | tf_op jit(solution)/shard_map/pallas_call | solution.py:335
  97.2 0.0 collective-permute-done.2.same_ref
  97.2 0.0 collective-permute-done.3.other_ref
  97.2 1.8 %shard_map.30.refs_0_ = f32[64,64,512]{2,1,0:T(8,128)} custom-call(bf16[8,64,128]{2,1,0:T(8,128)(2,1)S(1)} %collective-permute-done.2.same_ref, bf16[8,64,128]{2,1,0:T(8,128)(2,1)S(1)} %collective-permute-done.3.other_ref, bf16[64,64]{1,0:T(8,128)(2,1)S(1)} %get-tuple-element.19.ct_ref, ...), custom_call_target="tpu_custom_call", output_to_operand_aliasing={{}: (5, {})} | custom-call | flops 134217728 | bytes 4194304 | tf_op jit(solution)/shard_map/pallas_call | solution.py:335
  99.0 0.0 collective-permute-done.same_ref
  99.0 0.0 collective-permute-done.1.other_ref
  99.0 1.8 %shard_map.31 = f32[64,64,512]{2,1,0:T(8,128)} custom-call(bf16[8,64,128]{2,1,0:T(8,128)(2,1)S(1)} %collective-permute-done.same_ref, bf16[8,64,128]{2,1,0:T(8,128)(2,1)S(1)} %collective-permute-done.1.other_ref, bf16[64,64]{1,0:T(8,128)(2,1)S(1)} %get-tuple-element.19.ct_ref, ...), custom_call_target="tpu_custom_call", output_to_operand_aliasing={{}: (5, {})} | custom-call | flops 134217728 | bytes 4194304 | tf_op jit(solution)/shard_map/pallas_call | solution.py:335
Async XLA Ops:
  52.3 23.6 %collective-permute-start.4 = (bf16[8,64,128]{2,1,0:T(8,128)(2,1)S(1)}, bf16[8,64,128]{2,1,0:T(8,128)(2,1)S(1)}, u32[]{:S(2)}, u32[]{:S(2)}) collective-permute-start(bf16[8,64,128]{2,1,0:T(8,128)(2,1)S(1)} %get-tuple-element.25), channel_id=1, source_target_pairs={{2,4},{3,5},{4,2},{5,3},{10,12},{11,13},{12,10},{13,11},{18,20},{1... | collective-permute-start | bytes 393224 | tf_op jit(solution)/shard_map/ppermute | solution.py:321
  55.2 23.6 %collective-permute-start.6 = (bf16[8,64,128]{2,1,0:T(8,128)(2,1)S(1)}, bf16[8,64,128]{2,1,0:T(8,128)(2,1)S(1)}, u32[]{:S(2)}, u32[]{:S(2)}) collective-permute-start(bf16[8,64,128]{2,1,0:T(8,128)(2,1)S(1)} %get-tuple-element.27), channel_id=1, source_target_pairs={{2,4},{3,5},{4,2},{5,3},{10,12},{11,13},{12,10},{13,11},{18,20},{1... | collective-permute-start | bytes 393224 | tf_op jit(solution)/shard_map/ppermute | solution.py:321
  57.6 24.1 %collective-permute-start.7 = (bf16[8,64,128]{2,1,0:T(8,128)(2,1)S(1)}, bf16[8,64,128]{2,1,0:T(8,128)(2,1)S(1)}, u32[]{:S(2)}, u32[]{:S(2)}) collective-permute-start(bf16[8,64,128]{2,1,0:T(8,128)(2,1)S(1)} %get-tuple-element.28), channel_id=1, source_target_pairs={{2,5},{3,4},{4,3},{5,2},{10,13},{11,12},{12,11},{13,10},{18,21},{1... | collective-permute-start | bytes 393224 | tf_op jit(solution)/shard_map/ppermute | solution.py:321
  59.5 39.5 %collective-permute-start = (bf16[8,64,128]{2,1,0:T(8,128)(2,1)S(1)}, bf16[8,64,128]{2,1,0:T(8,128)(2,1)S(1)}, u32[]{:S(2)}, u32[]{:S(2)}) collective-permute-start(bf16[8,64,128]{2,1,0:T(8,128)(2,1)S(1)} %get-tuple-element.17), channel_id=1, source_target_pairs={{2,4},{3,5},{4,2},{5,3},{10,12},{11,13},{12,10},{13,11},{18,20},{1... | collective-permute-start | bytes 393224 | tf_op jit(solution)/shard_map/ppermute | solution.py:321
  62.4 36.6 %collective-permute-start.1 = (bf16[8,64,128]{2,1,0:T(8,128)(2,1)S(1)}, bf16[8,64,128]{2,1,0:T(8,128)(2,1)S(1)}, u32[]{:S(2)}, u32[]{:S(2)}) collective-permute-start(bf16[8,64,128]{2,1,0:T(8,128)(2,1)S(1)} %get-tuple-element.18), channel_id=1, source_target_pairs={{2,5},{3,4},{4,3},{5,2},{10,13},{11,12},{12,11},{13,10},{18,21},{1... | collective-permute-start | bytes 393224 | tf_op jit(solution)/shard_map/ppermute | solution.py:321
  75.8 21.3 %collective-permute-start.2 = (bf16[8,64,128]{2,1,0:T(8,128)(2,1)S(1)}, bf16[8,64,128]{2,1,0:T(8,128)(2,1)S(1)}, u32[]{:S(2)}, u32[]{:S(2)}) collective-permute-start(bf16[8,64,128]{2,1,0:T(8,128)(2,1)S(1)} %get-tuple-element.23), channel_id=1, source_target_pairs={{2,4},{3,5},{4,2},{5,3},{10,12},{11,13},{12,10},{13,11},{18,20},{1... | collective-permute-start | bytes 393224 | tf_op jit(solution)/shard_map/ppermute | solution.py:321
  78.8 18.4 %collective-permute-start.3 = (bf16[8,64,128]{2,1,0:T(8,128)(2,1)S(1)}, bf16[8,64,128]{2,1,0:T(8,128)(2,1)S(1)}, u32[]{:S(2)}, u32[]{:S(2)}) collective-permute-start(bf16[8,64,128]{2,1,0:T(8,128)(2,1)S(1)} %get-tuple-element.24), channel_id=1, source_target_pairs={{2,5},{3,4},{4,3},{5,2},{10,13},{11,12},{12,11},{13,10},{18,21},{1... | collective-permute-start | bytes 393224 | tf_op jit(solution)/shard_map/ppermute | solution.py:321
  81.7 13.6 %collective-permute-start.5 = (bf16[8,64,128]{2,1,0:T(8,128)(2,1)S(1)}, bf16[8,64,128]{2,1,0:T(8,128)(2,1)S(1)}, u32[]{:S(2)}, u32[]{:S(2)}) collective-permute-start(bf16[8,64,128]{2,1,0:T(8,128)(2,1)S(1)} %get-tuple-element.26), channel_id=1, source_target_pairs={{2,5},{3,4},{4,3},{5,2},{10,13},{11,12},{12,11},{13,10},{18,21},{1... | collective-permute-start | bytes 393224 | tf_op jit(solution)/shard_map/ppermute | solution.py:321

commit v2 on v1

--- a/solution.py
+++ b/solution.py
@@ -13,7 +13,7 @@
 ROWS = N // DEV
 COLS = N * N // DEV
 CHUNKS = COLS // 128
-EARLY = ((0, 1), (1, 1), (2, 2), (4, 4))
+EARLY = ((0, 1), (1, 1), (2, 1), (3, 1), (4, 2), (6, 2))
 LATER = ((0, 4), (4, 4))
 WHOLE = ((0, 8),)
 BF16 = jnp.bfloat16
@@ -49,6 +49,7 @@
         pl.semaphore_signal(barrier, inc=1, device_id={"dev": (me + k) % DEV}, device_id_type=pl.DeviceIdType.MESH)
 
     load_c.wait()
+    load_row(1).start()
     c = c_vm[...]
     nt = (((1,), (1,)), ((), ()))
     wide = (8 * N, 8 * N)
@@ -113,12 +114,12 @@
 
         pieces(p, h, l_vm[...], 32, put)
 
-    def chip_piece(to, lhs):
+    def chip_piece(p, to, lhs):
         def put(dest, q, columns, value):
-            send[2 * to + dest, 0, q, columns] = value
+            send[2 * to + dest, p, q, columns] = value
 
         for h in range(2):
-            pieces(0, h, lhs, 8, put)
+            pieces(p, h, lhs, 8, put)
 
     is_edge = jnp.logical_or(chip == 0, chip == 3)
     inward = jnp.where(chip < 2, 1, -1)
@@ -133,28 +134,26 @@
     l_vm[:128, :] = kron_rows(16 * first_chip, 16)
     for h in range(2):
         load_half(h).wait()
-    for later in (1, 2):
-        load_row(later).start()
-    chip_piece(first_chip, l_vm[:128, :])
+    load_row(2).start()
+    chip_piece(0, first_chip, l_vm[:128, :])
     pl.semaphore_wait(barrier, DEV - 1)
     start(EARLY[0], first_chip)
+    load_row(1).wait()
+    load_row(3).start()
+    chip_piece(1, first_chip, l_vm[:128, :])
+    start(EARLY[1], first_chip)
 
     l_vm[...] = kron_rows(0, N)
-
-    def l_rows(to):
-        return l_vm[pl.ds(pl.multiple_of(128 * to, 128), 128), :]
-
     second_chip = jnp.where(is_edge, far, outward)
-    chip_piece(second_chip, l_rows(second_chip))
-
-    @pl.when(jnp.logical_not(is_edge))
-    def _():
-        start(EARLY[0], outward)
-
     fourth_chip = jnp.where(is_edge, last, near)
-    chip_piece(fourth_chip, l_rows(fourth_chip))
-    chip_piece(chip, l_rows(chip))
-    group(EARLY[0], partner, me).start()
+    for p in range(2):
+        for to in (second_chip, fourth_chip, chip):
+            chip_piece(p, to, l_vm[pl.ds(pl.multiple_of(128 * to, 128), 128), :])
+        group(EARLY[p], partner, me).start()
+
+        @pl.when(jnp.logical_not(is_edge))
+        def _():
+            start(EARLY[p], outward)
 
     def make_row(p, carry):
         load_row(p).wait()
@@ -165,7 +164,7 @@
 
         for h in range(2):
             half_row(p, h)
-        for rows in EARLY[1:]:
+        for rows in EARLY[2:]:
             @pl.when(p == sum(rows) - 1)
             def _():
                 start(rows, beside)
@@ -178,7 +177,7 @@
 
         return carry
 
-    lax.fori_loop(1, ROWS, make_row, 0)
+    lax.fori_loop(2, ROWS, make_row, 0)
 
     @pl.when(is_edge)
     def _():

time: 101 us -> 101 us (level)
  the two profiles are of different devices: /device:TPU:15 before, /device:TPU:9 now
where the time goes in v2:
time: 101 us
  Pallas kernels  62.2 us (62%)
  starting transfers between devices  22.7 us (22%)
  waiting for transfers between devices  15.8 us (16%)
    pallas_call x1, Pallas kernels, local_transform(): pl.pallas_call(exchange_kernel, out_shape=outs, in_specs=[anywhere, anywh...  52.5 us
    ppermute x8, starting transfers between devices, local_transform(): pair.append(lax.ppermute(near[side * CHUNKS + chunk], 'dev', perm))  22.7 us
    ppermute x8, waiting for transfers between devices, local_transform(): pair.append(lax.ppermute(near[side * CHUNKS + chunk], 'dev', perm))  15.8 us
    pallas_call x4, Pallas kernels, local_transform(): pl.pallas_call(functools.partial(chunk_kernel, chunk), out_shape=sds((N,...  7.33 us
    pallas_call x1, Pallas kernels, local_transform(): pl.pallas_call(most_kernel, out_shape=sds((8, 8 * N, COLS), F32), in_spec...  2.34 us
  transfers between devices with their start and end apart: 8, of which 2 were waited for; matrix products, arithmetic and copies ran while one was open for 0% of the time, Pallas kernels for 8%

profile of v2, /device:TPU:9, one launch (start us, length us, event | category | flops | bytes accessed | tf_op | source)
XLA Modules:
  0.0 100.8 jit_solution(3376439184126945326)
XLA Ops:
  0.0 52.5 %exchange.1 = (bf16[8,512,512]{2,1,0:T(8,128)(2,1)S(1)}, bf16[512,512]{1,0:T(8,128)(2,1)S(1)}, bf16[512,128]{1,0:T(8,128)(2,1)S(1)}, bf16[64,64]{1,0:T(8,128)(2,...) custom-call(bf16[8,64,64,64]{3,2,1,0:T(8,128)(2,1)} %a_hbm.1, ...), custom_call_target="tpu_custom_call" | custom-call | tf_op jit(solution)/shard_map/exchange/pallas_call | solution.py:293
  52.5 2.8 %collective-permute-start.4 = (bf16[8,64,128]{2,1,0:T(8,128)(2,1)S(1)}, bf16[8,64,128]{2,1,0:T(8,128)(2,1)S(1)}, u32[]{:S(2)}, u32[]{:S(2)}) collective-permute-start(bf16[8,64,128]{2,1,0:T(8,128)(2,1)S(1)} %get-tuple-element.25), channel_id=1, source_target_pairs={{2,4},{3,5},{4,2},{5,3},{10,12},{11,13},{12,10},{13,11},{18,20},{1... | collective-permute-start | bytes 393224 | tf_op jit(solution)/shard_map/ppermute | solution.py:320
  55.3 2.5 %collective-permute-start.6 = (bf16[8,64,128]{2,1,0:T(8,128)(2,1)S(1)}, bf16[8,64,128]{2,1,0:T(8,128)(2,1)S(1)}, u32[]{:S(2)}, u32[]{:S(2)}) collective-permute-start(bf16[8,64,128]{2,1,0:T(8,128)(2,1)S(1)} %get-tuple-element.27), channel_id=1, source_target_pairs={{2,4},{3,5},{4,2},{5,3},{10,12},{11,13},{12,10},{13,11},{18,20},{1... | collective-permute-start | bytes 393224 | tf_op jit(solution)/shard_map/ppermute | solution.py:320
  57.8 1.9 %collective-permute-start.7 = (bf16[8,64,128]{2,1,0:T(8,128)(2,1)S(1)}, bf16[8,64,128]{2,1,0:T(8,128)(2,1)S(1)}, u32[]{:S(2)}, u32[]{:S(2)}) collective-permute-start(bf16[8,64,128]{2,1,0:T(8,128)(2,1)S(1)} %get-tuple-element.28), channel_id=1, source_target_pairs={{2,5},{3,4},{4,3},{5,2},{10,13},{11,12},{12,11},{13,10},{18,21},{1... | collective-permute-start | bytes 393224 | tf_op jit(solution)/shard_map/ppermute | solution.py:320
  59.8 2.8 %collective-permute-start = (bf16[8,64,128]{2,1,0:T(8,128)(2,1)S(1)}, bf16[8,64,128]{2,1,0:T(8,128)(2,1)S(1)}, u32[]{:S(2)}, u32[]{:S(2)}) collective-permute-start(bf16[8,64,128]{2,1,0:T(8,128)(2,1)S(1)} %get-tuple-element.17), channel_id=1, source_target_pairs={{2,4},{3,5},{4,2},{5,3},{10,12},{11,13},{12,10},{13,11},{18,20},{1... | collective-permute-start | bytes 393224 | tf_op jit(solution)/shard_map/ppermute | solution.py:320
  62.5 3.9 %collective-permute-start.1 = (bf16[8,64,128]{2,1,0:T(8,128)(2,1)S(1)}, bf16[8,64,128]{2,1,0:T(8,128)(2,1)S(1)}, u32[]{:S(2)}, u32[]{:S(2)}) collective-permute-start(bf16[8,64,128]{2,1,0:T(8,128)(2,1)S(1)} %get-tuple-element.18), channel_id=1, source_target_pairs={{2,5},{3,4},{4,3},{5,2},{10,13},{11,12},{12,11},{13,10},{18,21},{1... | collective-permute-start | bytes 393224 | tf_op jit(solution)/shard_map/ppermute | solution.py:320
  66.5 9.3 %collective-permute-done.4.same_ref = bf16[8,64,128]{2,1,0:T(8,128)(2,1)S(1)} collective-permute-done((bf16[8,64,128]{2,1,0:T(8,128)(2,1)S(1)}, bf16[8,64,128]{2,1,0:T(8,128)(2,1)S(1)}, u32[]{:S(2)}, u32[]{:S(2)}) %collective-permute-start.4) | collective-permute-done | bytes 131104 | tf_op jit(solution)/shard_map/ppermute | solution.py:320
  75.8 2.9 %collective-permute-start.2 = (bf16[8,64,128]{2,1,0:T(8,128)(2,1)S(1)}, bf16[8,64,128]{2,1,0:T(8,128)(2,1)S(1)}, u32[]{:S(2)}, u32[]{:S(2)}) collective-permute-start(bf16[8,64,128]{2,1,0:T(8,128)(2,1)S(1)} %get-tuple-element.23), channel_id=1, source_target_pairs={{2,4},{3,5},{4,2},{5,3},{10,12},{11,13},{12,10},{13,11},{18,20},{1... | collective-permute-start | bytes 393224 | tf_op jit(solution)/shard_map/ppermute | solution.py:320
  78.7 0.0 collective-permute-done.6.same_ref
  78.7 2.9 %collective-permute-start.3 = (bf16[8,64,128]{2,1,0:T(8,128)(2,1)S(1)}, bf16[8,64,128]{2,1,0:T(8,128)(2,1)S(1)}, u32[]{:S(2)}, u32[]{:S(2)}) collective-permute-start(bf16[8,64,128]{2,1,0:T(8,128)(2,1)S(1)} %get-tuple-element.24), channel_id=1, source_target_pairs={{2,5},{3,4},{4,3},{5,2},{10,13},{11,12},{12,11},{13,10},{18,21},{1... | collective-permute-start | bytes 393224 | tf_op jit(solution)/shard_map/ppermute | solution.py:320
  81.6 0.0 collective-permute-done.7.other_ref
  81.6 3.0 %collective-permute-start.5 = (bf16[8,64,128]{2,1,0:T(8,128)(2,1)S(1)}, bf16[8,64,128]{2,1,0:T(8,128)(2,1)S(1)}, u32[]{:S(2)}, u32[]{:S(2)}) collective-permute-start(bf16[8,64,128]{2,1,0:T(8,128)(2,1)S(1)} %get-tuple-element.26), channel_id=1, source_target_pairs={{2,5},{3,4},{4,3},{5,2},{10,13},{11,12},{12,11},{13,10},{18,21},{1... | collective-permute-start | bytes 393224 | tf_op jit(solution)/shard_map/ppermute | solution.py:320
  84.6 2.3 %most.1.most_ref = f32[8,512,512]{2,1,0:T(8,128)S(1)} custom-call(bf16[8,512,512]{2,1,0:T(8,128)(2,1)S(1)} %get-tuple-element.21.g_ref, bf16[512,512]{1,0:T(8,128)(2,1)S(1)} %get-tuple-element.22.l4_ref), custom_call_target="tpu_custom_call" | custom-call | flops 2147483648 | bytes 12582912 | tf_op jit(solution)/shard_map/most/pallas_call | solution.py:322
  86.9 1.8 %shard_map.28.refs_0_ = f32[64,64,512]{2,1,0:T(8,128)} custom-call(bf16[8,64,128]{2,1,0:T(8,128)(2,1)S(1)} %collective-permute-done.6.same_ref, bf16[8,64,128]{2,1,0:T(8,128)(2,1)S(1)} %collective-permute-done.7.other_ref, bf16[64,64]{1,0:T(8,128)(2,1)S(1)} %get-tuple-element.19.ct_ref, bf16[512,128]{1,0:T(8,128)(2,1)S(1)} %get-tuple-element.20.l4n_ref, ...), custom_call_target="tpu_custom_call" | custom-call | flops 134217728 | bytes 4194304 | tf_op jit(solution)/shard_map/pallas_call | solution.py:334
  88.8 6.5 %collective-permute-done.5.other_ref = bf16[8,64,128]{2,1,0:T(8,128)(2,1)S(1)} collective-permute-done((bf16[8,64,128]{2,1,0:T(8,128)(2,1)S(1)}, bf16[8,64,128]{2,1,0:T(8,128)(2,1)S(1)}, u32[]{:S(2)}, u32[]{:S(2)}) %collective-permute-start.5) | collective-permute-done | bytes 131104 | tf_op jit(solution)/shard_map/ppermute | solution.py:320
  95.2 1.8 %shard_map.29.refs_0_ = f32[64,64,512]{2,1,0:T(8,128)} custom-call(bf16[8,64,128]{2,1,0:T(8,128)(2,1)S(1)} %collective-permute-done.4.same_ref, bf16[8,64,128]{2,1,0:T(8,128)(2,1)S(1)} %collective-permute-done.5.other_ref, bf16[64,64]{1,0:T(8,128)(2,1)S(1)} %get-tuple-element.19.ct_ref, ...), custom_call_target="tpu_custom_call", output_to_operand_aliasing={{}: (5, {})} | custom-call | flops 134217728 | bytes 4194304 | tf_op jit(solution)/shard_map/pallas_call | solution.py:334
  97.1 0.0 collective-permute-done.2.same_ref
  97.1 0.0 collective-permute-done.3.other_ref
  97.1 1.8 %shard_map.30.refs_0_ = f32[64,64,512]{2,1,0:T(8,128)} custom-call(bf16[8,64,128]{2,1,0:T(8,128)(2,1)S(1)} %collective-permute-done.2.same_ref, bf16[8,64,128]{2,1,0:T(8,128)(2,1)S(1)} %collective-permute-done.3.other_ref, bf16[64,64]{1,0:T(8,128)(2,1)S(1)} %get-tuple-element.19.ct_ref, ...), custom_call_target="tpu_custom_call", output_to_operand_aliasing={{}: (5, {})} | custom-call | flops 134217728 | bytes 4194304 | tf_op jit(solution)/shard_map/pallas_call | solution.py:334
  98.9 0.0 collective-permute-done.same_ref
  98.9 0.0 collective-permute-done.1.other_ref
  98.9 1.8 %shard_map.31 = f32[64,64,512]{2,1,0:T(8,128)} custom-call(bf16[8,64,128]{2,1,0:T(8,128)(2,1)S(1)} %collective-permute-done.same_ref, bf16[8,64,128]{2,1,0:T(8,128)(2,1)S(1)} %collective-permute-done.1.other_ref, bf16[64,64]{1,0:T(8,128)(2,1)S(1)} %get-tuple-element.19.ct_ref, ...), custom_call_target="tpu_custom_call", output_to_operand_aliasing={{}: (5, {})} | custom-call | flops 134217728 | bytes 4194304 | tf_op jit(solution)/shard_map/pallas_call | solution.py:334
Async XLA Ops:
  52.5 23.2 %collective-permute-start.4 = (bf16[8,64,128]{2,1,0:T(8,128)(2,1)S(1)}, bf16[8,64,128]{2,1,0:T(8,128)(2,1)S(1)}, u32[]{:S(2)}, u32[]{:S(2)}) collective-permute-start(bf16[8,64,128]{2,1,0:T(8,128)(2,1)S(1)} %get-tuple-element.25), channel_id=1, source_target_pairs={{2,4},{3,5},{4,2},{5,3},{10,12},{11,13},{12,10},{13,11},{18,20},{1... | collective-permute-start | bytes 393224 | tf_op jit(solution)/shard_map/ppermute | solution.py:320
  55.3 23.4 %collective-permute-start.6 = (bf16[8,64,128]{2,1,0:T(8,128)(2,1)S(1)}, bf16[8,64,128]{2,1,0:T(8,128)(2,1)S(1)}, u32[]{:S(2)}, u32[]{:S(2)}) collective-permute-start(bf16[8,64,128]{2,1,0:T(8,128)(2,1)S(1)} %get-tuple-element.27), channel_id=1, source_target_pairs={{2,4},{3,5},{4,2},{5,3},{10,12},{11,13},{12,10},{13,11},{18,20},{1... | collective-permute-start | bytes 393224 | tf_op jit(solution)/shard_map/ppermute | solution.py:320
  57.8 23.8 %collective-permute-start.7 = (bf16[8,64,128]{2,1,0:T(8,128)(2,1)S(1)}, bf16[8,64,128]{2,1,0:T(8,128)(2,1)S(1)}, u32[]{:S(2)}, u32[]{:S(2)}) collective-permute-start(bf16[8,64,128]{2,1,0:T(8,128)(2,1)S(1)} %get-tuple-element.28), channel_id=1, source_target_pairs={{2,5},{3,4},{4,3},{5,2},{10,13},{11,12},{12,11},{13,10},{18,21},{1... | collective-permute-start | bytes 393224 | tf_op jit(solution)/shard_map/ppermute | solution.py:320
  59.8 39.2 %collective-permute-start = (bf16[8,64,128]{2,1,0:T(8,128)(2,1)S(1)}, bf16[8,64,128]{2,1,0:T(8,128)(2,1)S(1)}, u32[]{:S(2)}, u32[]{:S(2)}) collective-permute-start(bf16[8,64,128]{2,1,0:T(8,128)(2,1)S(1)} %get-tuple-element.17), channel_id=1, source_target_pairs={{2,4},{3,5},{4,2},{5,3},{10,12},{11,13},{12,10},{13,11},{18,20},{1... | collective-permute-start | bytes 393224 | tf_op jit(solution)/shard_map/ppermute | solution.py:320
  62.5 36.4 %collective-permute-start.1 = (bf16[8,64,128]{2,1,0:T(8,128)(2,1)S(1)}, bf16[8,64,128]{2,1,0:T(8,128)(2,1)S(1)}, u32[]{:S(2)}, u32[]{:S(2)}) collective-permute-start(bf16[8,64,128]{2,1,0:T(8,128)(2,1)S(1)} %get-tuple-element.18), channel_id=1, source_target_pairs={{2,5},{3,4},{4,3},{5,2},{10,13},{11,12},{12,11},{13,10},{18,21},{1... | collective-permute-start | bytes 393224 | tf_op jit(solution)/shard_map/ppermute | solution.py:320
  75.8 21.3 %collective-permute-start.2 = (bf16[8,64,128]{2,1,0:T(8,128)(2,1)S(1)}, bf16[8,64,128]{2,1,0:T(8,128)(2,1)S(1)}, u32[]{:S(2)}, u32[]{:S(2)}) collective-permute-start(bf16[8,64,128]{2,1,0:T(8,128)(2,1)S(1)} %get-tuple-element.23), channel_id=1, source_target_pairs={{2,4},{3,5},{4,2},{5,3},{10,12},{11,13},{12,10},{13,11},{18,20},{1... | collective-permute-start | bytes 393224 | tf_op jit(solution)/shard_map/ppermute | solution.py:320
  78.7 18.4 %collective-permute-start.3 = (bf16[8,64,128]{2,1,0:T(8,128)(2,1)S(1)}, bf16[8,64,128]{2,1,0:T(8,128)(2,1)S(1)}, u32[]{:S(2)}, u32[]{:S(2)}) collective-permute-start(bf16[8,64,128]{2,1,0:T(8,128)(2,1)S(1)} %get-tuple-element.24), channel_id=1, source_target_pairs={{2,5},{3,4},{4,3},{5,2},{10,13},{11,12},{12,11},{13,10},{18,21},{1... | collective-permute-start | bytes 393224 | tf_op jit(solution)/shard_map/ppermute | solution.py:320
  81.6 13.6 %collective-permute-start.5 = (bf16[8,64,128]{2,1,0:T(8,128)(2,1)S(1)}, bf16[8,64,128]{2,1,0:T(8,128)(2,1)S(1)}, u32[]{:S(2)}, u32[]{:S(2)}) collective-permute-start(bf16[8,64,128]{2,1,0:T(8,128)(2,1)S(1)} %get-tuple-element.26), channel_id=1, source_target_pairs={{2,5},{3,4},{4,3},{5,2},{10,13},{11,12},{12,11},{13,10},{18,21},{1... | collective-permute-start | bytes 393224 | tf_op jit(solution)/shard_map/ppermute | solution.py:320

commit v3 on v2

--- a/solution.py
+++ b/solution.py
@@ -263,18 +263,25 @@
     core = lax.axis_index("dev") % 2
     for side, ref in ((core, same_ref), (1 - core, other_ref)):
         for p in range(0, ROWS, 2):
-            g0 = jnp.dot(ct_ref[...], ref[p], preferred_element_type=F32).reshape(8, 8, 128)
-            g1 = jnp.dot(ct_ref[...], ref[p + 1], preferred_element_type=F32).reshape(8, 8, 128)
+            both = jnp.concatenate([ref[p], ref[p + 1]], axis=1)
+            g = jnp.dot(ct_ref[...], both, preferred_element_type=F32)
+            g0 = g[:, :128].reshape(8, 8, 128)
+            g1 = g[:, 128:].reshape(8, 8, 128)
             at = pl.multiple_of(N * side + 8 * p, 16)
             g_vm[:, pl.ds(at, 16), :] = jnp.concatenate([g0, g1], axis=1).astype(BF16)
 
     def put(ag):
         return pltpu.make_async_copy(v_vm.at[ag], v_hbm.at[:, pl.ds(8 * ag, 8), pl.ds(128 * chunk, 128)], v_sem.at[ag])
 
-    for ag in range(8):
-        part = jnp.dot(l4n_ref[...], g_vm[ag], preferred_element_type=F32)
-        v_vm[ag] = (part + most_ref[ag, :, 128 * chunk:128 * chunk + 128]).reshape(N, 8, 128)
-        put(ag).start()
+    for ag in range(0, 8, 2):
+        both = jnp.concatenate([g_vm[ag], g_vm[ag + 1]], axis=1)
+        for m in range(2):
+            part = jnp.dot(l4n_ref[256 * m:256 * m + 256, :], both, preferred_element_type=F32)
+            for k in range(2):
+                most = most_ref[ag + k, 256 * m:256 * m + 256, 128 * chunk:128 * chunk + 128]
+                v_vm[ag + k, 32 * m:32 * m + 32] = (part[:, 128 * k:128 * k + 128] + most).reshape(N // 2, 8, 128)
+        for k in range(2):
+            put(ag + k).start()
     for ag in range(8):
         put(ag).wait()
 

time: 101 us -> 101 us (level)
  the two profiles are of different devices: /device:TPU:9 before, /device:TPU:15 now
where the time goes in v3:
time: 101 us
  Pallas kernels  62 us (61%)
  starting transfers between devices  22.7 us (22%)
  waiting for transfers between devices  15.8 us (16%)
    pallas_call x1, Pallas kernels, local_transform(): pl.pallas_call(exchange_kernel, out_shape=outs, in_specs=[anywhere, anywh...  52.5 us
    ppermute x8, starting transfers between devices, local_transform(): pair.append(lax.ppermute(near[side * CHUNKS + chunk], 'dev', perm))  22.7 us
    ppermute x8, waiting for transfers between devices, local_transform(): pair.append(lax.ppermute(near[side * CHUNKS + chunk], 'dev', perm))  15.8 us
    pallas_call x4, Pallas kernels, local_transform(): pl.pallas_call(functools.partial(chunk_kernel, chunk), out_shape=sds((N,...  7.18 us
    pallas_call x1, Pallas kernels, local_transform(): pl.pallas_call(most_kernel, out_shape=sds((8, 8 * N, COLS), F32), in_spec...  2.34 us
  transfers between devices with their start and end apart: 8, of which 2 were waited for; matrix products, arithmetic and copies ran while one was open for 0% of the time, Pallas kernels for 8%

profile of v3, /device:TPU:15, one launch (start us, length us, event | category | flops | bytes accessed | tf_op | source)
XLA Modules:
  0.0 100.7 jit_solution(7006104327936614734)
XLA Ops:
  0.0 52.5 %exchange.1 = (bf16[8,512,512]{2,1,0:T(8,128)(2,1)S(1)}, bf16[512,512]{1,0:T(8,128)(2,1)S(1)}, bf16[512,128]{1,0:T(8,128)(2,1)S(1)}, bf16[64,64]{1,0:T(8,128)(2,...) custom-call(bf16[8,64,64,64]{3,2,1,0:T(8,128)(2,1)} %a_hbm.1, ...), custom_call_target="tpu_custom_call" | custom-call | tf_op jit(solution)/shard_map/exchange/pallas_call | solution.py:300
  52.5 2.8 %collective-permute-start.4 = (bf16[8,64,128]{2,1,0:T(8,128)(2,1)S(1)}, bf16[8,64,128]{2,1,0:T(8,128)(2,1)S(1)}, u32[]{:S(2)}, u32[]{:S(2)}) collective-permute-start(bf16[8,64,128]{2,1,0:T(8,128)(2,1)S(1)} %get-tuple-element.25), channel_id=1, source_target_pairs={{2,4},{3,5},{4,2},{5,3},{10,12},{11,13},{12,10},{13,11},{18,20},{1... | collective-permute-start | bytes 393224 | tf_op jit(solution)/shard_map/ppermute | solution.py:327
  55.3 2.5 %collective-permute-start.6 = (bf16[8,64,128]{2,1,0:T(8,128)(2,1)S(1)}, bf16[8,64,128]{2,1,0:T(8,128)(2,1)S(1)}, u32[]{:S(2)}, u32[]{:S(2)}) collective-permute-start(bf16[8,64,128]{2,1,0:T(8,128)(2,1)S(1)} %get-tuple-element.27), channel_id=1, source_target_pairs={{2,4},{3,5},{4,2},{5,3},{10,12},{11,13},{12,10},{13,11},{18,20},{1... | collective-permute-start | bytes 393224 | tf_op jit(solution)/shard_map/ppermute | solution.py:327
  57.8 1.9 %collective-permute-start.7 = (bf16[8,64,128]{2,1,0:T(8,128)(2,1)S(1)}, bf16[8,64,128]{2,1,0:T(8,128)(2,1)S(1)}, u32[]{:S(2)}, u32[]{:S(2)}) collective-permute-start(bf16[8,64,128]{2,1,0:T(8,128)(2,1)S(1)} %get-tuple-element.28), channel_id=1, source_target_pairs={{2,5},{3,4},{4,3},{5,2},{10,13},{11,12},{12,11},{13,10},{18,21},{1... | collective-permute-start | bytes 393224 | tf_op jit(solution)/shard_map/ppermute | solution.py:327
  59.7 2.8 %collective-permute-start = (bf16[8,64,128]{2,1,0:T(8,128)(2,1)S(1)}, bf16[8,64,128]{2,1,0:T(8,128)(2,1)S(1)}, u32[]{:S(2)}, u32[]{:S(2)}) collective-permute-start(bf16[8,64,128]{2,1,0:T(8,128)(2,1)S(1)} %get-tuple-element.17), channel_id=1, source_target_pairs={{2,4},{3,5},{4,2},{5,3},{10,12},{11,13},{12,10},{13,11},{18,20},{1... | collective-permute-start | bytes 393224 | tf_op jit(solution)/shard_map/ppermute | solution.py:327
  62.5 3.9 %collective-permute-start.1 = (bf16[8,64,128]{2,1,0:T(8,128)(2,1)S(1)}, bf16[8,64,128]{2,1,0:T(8,128)(2,1)S(1)}, u32[]{:S(2)}, u32[]{:S(2)}) collective-permute-start(bf16[8,64,128]{2,1,0:T(8,128)(2,1)S(1)} %get-tuple-element.18), channel_id=1, source_target_pairs={{2,5},{3,4},{4,3},{5,2},{10,13},{11,12},{12,11},{13,10},{18,21},{1... | collective-permute-start | bytes 393224 | tf_op jit(solution)/shard_map/ppermute | solution.py:327
  66.4 9.3 %collective-permute-done.4.same_ref = bf16[8,64,128]{2,1,0:T(8,128)(2,1)S(1)} collective-permute-done((bf16[8,64,128]{2,1,0:T(8,128)(2,1)S(1)}, bf16[8,64,128]{2,1,0:T(8,128)(2,1)S(1)}, u32[]{:S(2)}, u32[]{:S(2)}) %collective-permute-start.4) | collective-permute-done | bytes 131104 | tf_op jit(solution)/shard_map/ppermute | solution.py:327
  75.8 2.9 %collective-permute-start.2 = (bf16[8,64,128]{2,1,0:T(8,128)(2,1)S(1)}, bf16[8,64,128]{2,1,0:T(8,128)(2,1)S(1)}, u32[]{:S(2)}, u32[]{:S(2)}) collective-permute-start(bf16[8,64,128]{2,1,0:T(8,128)(2,1)S(1)} %get-tuple-element.23), channel_id=1, source_target_pairs={{2,4},{3,5},{4,2},{5,3},{10,12},{11,13},{12,10},{13,11},{18,20},{1... | collective-permute-start | bytes 393224 | tf_op jit(solution)/shard_map/ppermute | solution.py:327
  78.7 0.0 collective-permute-done.6.same_ref
  78.7 2.9 %collective-permute-start.3 = (bf16[8,64,128]{2,1,0:T(8,128)(2,1)S(1)}, bf16[8,64,128]{2,1,0:T(8,128)(2,1)S(1)}, u32[]{:S(2)}, u32[]{:S(2)}) collective-permute-start(bf16[8,64,128]{2,1,0:T(8,128)(2,1)S(1)} %get-tuple-element.24), channel_id=1, source_target_pairs={{2,5},{3,4},{4,3},{5,2},{10,13},{11,12},{12,11},{13,10},{18,21},{1... | collective-permute-start | bytes 393224 | tf_op jit(solution)/shard_map/ppermute | solution.py:327
  81.6 0.0 collective-permute-done.7.other_ref
  81.6 3.0 %collective-permute-start.5 = (bf16[8,64,128]{2,1,0:T(8,128)(2,1)S(1)}, bf16[8,64,128]{2,1,0:T(8,128)(2,1)S(1)}, u32[]{:S(2)}, u32[]{:S(2)}) collective-permute-start(bf16[8,64,128]{2,1,0:T(8,128)(2,1)S(1)} %get-tuple-element.26), channel_id=1, source_target_pairs={{2,5},{3,4},{4,3},{5,2},{10,13},{11,12},{12,11},{13,10},{18,21},{1... | collective-permute-start | bytes 393224 | tf_op jit(solution)/shard_map/ppermute | solution.py:327
  84.6 2.3 %most.1.most_ref = f32[8,512,512]{2,1,0:T(8,128)S(1)} custom-call(bf16[8,512,512]{2,1,0:T(8,128)(2,1)S(1)} %get-tuple-element.21.g_ref, bf16[512,512]{1,0:T(8,128)(2,1)S(1)} %get-tuple-element.22.l4_ref), custom_call_target="tpu_custom_call" | custom-call | flops 2147483648 | bytes 12582912 | tf_op jit(solution)/shard_map/most/pallas_call | solution.py:329
  86.9 1.8 %shard_map.28.refs_0_ = f32[64,64,512]{2,1,0:T(8,128)} custom-call(bf16[8,64,128]{2,1,0:T(8,128)(2,1)S(1)} %collective-permute-done.6.same_ref, bf16[8,64,128]{2,1,0:T(8,128)(2,1)S(1)} %collective-permute-done.7.other_ref, bf16[64,64]{1,0:T(8,128)(2,1)S(1)} %get-tuple-element.19.ct_ref, bf16[512,128]{1,0:T(8,128)(2,1)S(1)} %get-tuple-element.20.l4n_ref, ...), custom_call_target="tpu_custom_call" | custom-call | flops 134217728 | bytes 4194304 | tf_op jit(solution)/shard_map/pallas_call | solution.py:341
  88.7 6.5 %collective-permute-done.5.other_ref = bf16[8,64,128]{2,1,0:T(8,128)(2,1)S(1)} collective-permute-done((bf16[8,64,128]{2,1,0:T(8,128)(2,1)S(1)}, bf16[8,64,128]{2,1,0:T(8,128)(2,1)S(1)}, u32[]{:S(2)}, u32[]{:S(2)}) %collective-permute-start.5) | collective-permute-done | bytes 131104 | tf_op jit(solution)/shard_map/ppermute | solution.py:327
  95.2 1.8 %shard_map.29.refs_0_ = f32[64,64,512]{2,1,0:T(8,128)} custom-call(bf16[8,64,128]{2,1,0:T(8,128)(2,1)S(1)} %collective-permute-done.4.same_ref, bf16[8,64,128]{2,1,0:T(8,128)(2,1)S(1)} %collective-permute-done.5.other_ref, bf16[64,64]{1,0:T(8,128)(2,1)S(1)} %get-tuple-element.19.ct_ref, ...), custom_call_target="tpu_custom_call", output_to_operand_aliasing={{}: (5, {})} | custom-call | flops 134217728 | bytes 4194304 | tf_op jit(solution)/shard_map/pallas_call | solution.py:341
  97.0 0.0 collective-permute-done.2.same_ref
  97.0 0.0 collective-permute-done.3.other_ref
  97.0 1.8 %shard_map.30.refs_0_ = f32[64,64,512]{2,1,0:T(8,128)} custom-call(bf16[8,64,128]{2,1,0:T(8,128)(2,1)S(1)} %collective-permute-done.2.same_ref, bf16[8,64,128]{2,1,0:T(8,128)(2,1)S(1)} %collective-permute-done.3.other_ref, bf16[64,64]{1,0:T(8,128)(2,1)S(1)} %get-tuple-element.19.ct_ref, ...), custom_call_target="tpu_custom_call", output_to_operand_aliasing={{}: (5, {})} | custom-call | flops 134217728 | bytes 4194304 | tf_op jit(solution)/shard_map/pallas_call | solution.py:341
  98.9 0.0 collective-permute-done.same_ref
  98.9 0.0 collective-permute-done.1.other_ref
  98.9 1.8 %shard_map.31 = f32[64,64,512]{2,1,0:T(8,128)} custom-call(bf16[8,64,128]{2,1,0:T(8,128)(2,1)S(1)} %collective-permute-done.same_ref, bf16[8,64,128]{2,1,0:T(8,128)(2,1)S(1)} %collective-permute-done.1.other_ref, bf16[64,64]{1,0:T(8,128)(2,1)S(1)} %get-tuple-element.19.ct_ref, ...), custom_call_target="tpu_custom_call", output_to_operand_aliasing={{}: (5, {})} | custom-call | flops 134217728 | bytes 4194304 | tf_op jit(solution)/shard_map/pallas_call | solution.py:341
Async XLA Ops:
  52.5 23.2 %collective-permute-start.4 = (bf16[8,64,128]{2,1,0:T(8,128)(2,1)S(1)}, bf16[8,64,128]{2,1,0:T(8,128)(2,1)S(1)}, u32[]{:S(2)}, u32[]{:S(2)}) collective-permute-start(bf16[8,64,128]{2,1,0:T(8,128)(2,1)S(1)} %get-tuple-element.25), channel_id=1, source_target_pairs={{2,4},{3,5},{4,2},{5,3},{10,12},{11,13},{12,10},{13,11},{18,20},{1... | collective-permute-start | bytes 393224 | tf_op jit(solution)/shard_map/ppermute | solution.py:327
  55.3 23.4 %collective-permute-start.6 = (bf16[8,64,128]{2,1,0:T(8,128)(2,1)S(1)}, bf16[8,64,128]{2,1,0:T(8,128)(2,1)S(1)}, u32[]{:S(2)}, u32[]{:S(2)}) collective-permute-start(bf16[8,64,128]{2,1,0:T(8,128)(2,1)S(1)} %get-tuple-element.27), channel_id=1, source_target_pairs={{2,4},{3,5},{4,2},{5,3},{10,12},{11,13},{12,10},{13,11},{18,20},{1... | collective-permute-start | bytes 393224 | tf_op jit(solution)/shard_map/ppermute | solution.py:327
  57.8 23.8 %collective-permute-start.7 = (bf16[8,64,128]{2,1,0:T(8,128)(2,1)S(1)}, bf16[8,64,128]{2,1,0:T(8,128)(2,1)S(1)}, u32[]{:S(2)}, u32[]{:S(2)}) collective-permute-start(bf16[8,64,128]{2,1,0:T(8,128)(2,1)S(1)} %get-tuple-element.28), channel_id=1, source_target_pairs={{2,5},{3,4},{4,3},{5,2},{10,13},{11,12},{12,11},{13,10},{18,21},{1... | collective-permute-start | bytes 393224 | tf_op jit(solution)/shard_map/ppermute | solution.py:327
  59.7 39.1 %collective-permute-start = (bf16[8,64,128]{2,1,0:T(8,128)(2,1)S(1)}, bf16[8,64,128]{2,1,0:T(8,128)(2,1)S(1)}, u32[]{:S(2)}, u32[]{:S(2)}) collective-permute-start(bf16[8,64,128]{2,1,0:T(8,128)(2,1)S(1)} %get-tuple-element.17), channel_id=1, source_target_pairs={{2,4},{3,5},{4,2},{5,3},{10,12},{11,13},{12,10},{13,11},{18,20},{1... | collective-permute-start | bytes 393224 | tf_op jit(solution)/shard_map/ppermute | solution.py:327
  62.5 36.4 %collective-permute-start.1 = (bf16[8,64,128]{2,1,0:T(8,128)(2,1)S(1)}, bf16[8,64,128]{2,1,0:T(8,128)(2,1)S(1)}, u32[]{:S(2)}, u32[]{:S(2)}) collective-permute-start(bf16[8,64,128]{2,1,0:T(8,128)(2,1)S(1)} %get-tuple-element.18), channel_id=1, source_target_pairs={{2,5},{3,4},{4,3},{5,2},{10,13},{11,12},{12,11},{13,10},{18,21},{1... | collective-permute-start | bytes 393224 | tf_op jit(solution)/shard_map/ppermute | solution.py:327
  75.8 21.3 %collective-permute-start.2 = (bf16[8,64,128]{2,1,0:T(8,128)(2,1)S(1)}, bf16[8,64,128]{2,1,0:T(8,128)(2,1)S(1)}, u32[]{:S(2)}, u32[]{:S(2)}) collective-permute-start(bf16[8,64,128]{2,1,0:T(8,128)(2,1)S(1)} %get-tuple-element.23), channel_id=1, source_target_pairs={{2,4},{3,5},{4,2},{5,3},{10,12},{11,13},{12,10},{13,11},{18,20},{1... | collective-permute-start | bytes 393224 | tf_op jit(solution)/shard_map/ppermute | solution.py:327
  78.7 18.3 %collective-permute-start.3 = (bf16[8,64,128]{2,1,0:T(8,128)(2,1)S(1)}, bf16[8,64,128]{2,1,0:T(8,128)(2,1)S(1)}, u32[]{:S(2)}, u32[]{:S(2)}) collective-permute-start(bf16[8,64,128]{2,1,0:T(8,128)(2,1)S(1)} %get-tuple-element.24), channel_id=1, source_target_pairs={{2,5},{3,4},{4,3},{5,2},{10,13},{11,12},{12,11},{13,10},{18,21},{1... | collective-permute-start | bytes 393224 | tf_op jit(solution)/shard_map/ppermute | solution.py:327
  81.6 13.6 %collective-permute-start.5 = (bf16[8,64,128]{2,1,0:T(8,128)(2,1)S(1)}, bf16[8,64,128]{2,1,0:T(8,128)(2,1)S(1)}, u32[]{:S(2)}, u32[]{:S(2)}) collective-permute-start(bf16[8,64,128]{2,1,0:T(8,128)(2,1)S(1)} %get-tuple-element.26), channel_id=1, source_target_pairs={{2,5},{3,4},{4,3},{5,2},{10,13},{11,12},{12,11},{13,10},{18,21},{1... | collective-permute-start | bytes 393224 | tf_op jit(solution)/shard_map/ppermute | solution.py:327

commit v4 on v3

--- a/solution.py
+++ b/solution.py
@@ -270,20 +270,22 @@
             at = pl.multiple_of(N * side + 8 * p, 16)
             g_vm[:, pl.ds(at, 16), :] = jnp.concatenate([g0, g1], axis=1).astype(BF16)
 
-    def put(ag):
-        return pltpu.make_async_copy(v_vm.at[ag], v_hbm.at[:, pl.ds(8 * ag, 8), pl.ds(128 * chunk, 128)], v_sem.at[ag])
-
-    for ag in range(0, 8, 2):
-        both = jnp.concatenate([g_vm[ag], g_vm[ag + 1]], axis=1)
-        for m in range(2):
-            part = jnp.dot(l4n_ref[256 * m:256 * m + 256, :], both, preferred_element_type=F32)
+    def put(m):
+        part = pl.ds(16 * m, 16)
+        return pltpu.make_async_copy(v_vm.at[part], v_hbm.at[part, :, pl.ds(128 * chunk, 128)], v_sem.at[m])
+
+    for m in range(4):
+        rows = slice(128 * m, 128 * m + 128)
+        for ag in range(0, 8, 2):
+            both = jnp.concatenate([g_vm[ag], g_vm[ag + 1]], axis=1)
+            part = jnp.dot(l4n_ref[rows, :], both, preferred_element_type=F32)
             for k in range(2):
-                most = most_ref[ag + k, 256 * m:256 * m + 256, 128 * chunk:128 * chunk + 128]
-                v_vm[ag + k, 32 * m:32 * m + 32] = (part[:, 128 * k:128 * k + 128] + most).reshape(N // 2, 8, 128)
-        for k in range(2):
-            put(ag + k).start()
-    for ag in range(8):
-        put(ag).wait()
+                most = most_ref[ag + k, rows, 128 * chunk:128 * chunk + 128]
+                value = (part[:, 128 * k:128 * k + 128] + most).reshape(16, 8, 128)
+                v_vm[16 * m:16 * m + 16, 8 * (ag + k):8 * (ag + k) + 8, :] = value
+        put(m).start()
+    for m in range(4):
+        put(m).wait()
 
 
 def solution(mesh):
@@ -345,8 +347,8 @@
                 out_specs=anywhere,
                 scratch_shapes=[
                     pltpu.VMEM((8, 2 * N, 128), BF16),
-                    pltpu.VMEM((8, N, 8, 128), F32),
-                    pltpu.SemaphoreType.DMA((8,)),
+                    pltpu.VMEM((N, N, 128), F32),
+                    pltpu.SemaphoreType.DMA((4,)),
                 ],
                 input_output_aliases={} if v is None else {5: 0},
                 compiler_params=pltpu.CompilerParams(vmem_limit_bytes=12 * 2**20),

time: 101 us -> 101 us (level)
  the two profiles are of different devices: /device:TPU:15 before, /device:TPU:13 now
where the time goes in v4:
time: 101 us
  Pallas kernels  62 us (61%)
  starting transfers between devices  22.7 us (22%)
  waiting for transfers between devices  15.8 us (16%)
    pallas_call x1, Pallas kernels, local_transform(): pl.pallas_call(exchange_kernel, out_shape=outs, in_specs=[anywhere, anywh...  52.5 us
    ppermute x8, starting transfers between devices, local_transform(): pair.append(lax.ppermute(near[side * CHUNKS + chunk], 'dev', perm))  22.7 us
    ppermute x8, waiting for transfers between devices, local_transform(): pair.append(lax.ppermute(near[side * CHUNKS + chunk], 'dev', perm))  15.8 us
    pallas_call x4, Pallas kernels, local_transform(): pl.pallas_call(functools.partial(chunk_kernel, chunk), out_shape=sds((N,...  7.13 us
    pallas_call x1, Pallas kernels, local_transform(): pl.pallas_call(most_kernel, out_shape=sds((8, 8 * N, COLS), F32), in_spec...  2.34 us
  transfers between devices with their start and end apart: 8, of which 2 were waited for; matrix products, arithmetic and copies ran while one was open for 0% of the time, Pallas kernels for 8%

profile of v4, /device:TPU:13, one launch (start us, length us, event | category | flops | bytes accessed | tf_op | source)
XLA Modules:
  0.0 100.6 jit_solution(1387850899875452686)
XLA Ops:
  0.0 52.5 %exchange.1 = (bf16[8,512,512]{2,1,0:T(8,128)(2,1)S(1)}, bf16[512,512]{1,0:T(8,128)(2,1)S(1)}, bf16[512,128]{1,0:T(8,128)(2,1)S(1)}, bf16[64,64]{1,0:T(8,128)(2,...) custom-call(bf16[8,64,64,64]{3,2,1,0:T(8,128)(2,1)} %a_hbm.1, ...), custom_call_target="tpu_custom_call" | custom-call | tf_op jit(solution)/shard_map/exchange/pallas_call | solution.py:302
  52.5 2.8 %collective-permute-start.4 = (bf16[8,64,128]{2,1,0:T(8,128)(2,1)S(1)}, bf16[8,64,128]{2,1,0:T(8,128)(2,1)S(1)}, u32[]{:S(2)}, u32[]{:S(2)}) collective-permute-start(bf16[8,64,128]{2,1,0:T(8,128)(2,1)S(1)} %get-tuple-element.25), channel_id=1, source_target_pairs={{2,4},{3,5},{4,2},{5,3},{10,12},{11,13},{12,10},{13,11},{18,20},{1... | collective-permute-start | bytes 393224 | tf_op jit(solution)/shard_map/ppermute | solution.py:329
  55.3 2.5 %collective-permute-start.6 = (bf16[8,64,128]{2,1,0:T(8,128)(2,1)S(1)}, bf16[8,64,128]{2,1,0:T(8,128)(2,1)S(1)}, u32[]{:S(2)}, u32[]{:S(2)}) collective-permute-start(bf16[8,64,128]{2,1,0:T(8,128)(2,1)S(1)} %get-tuple-element.27), channel_id=1, source_target_pairs={{2,4},{3,5},{4,2},{5,3},{10,12},{11,13},{12,10},{13,11},{18,20},{1... | collective-permute-start | bytes 393224 | tf_op jit(solution)/shard_map/ppermute | solution.py:329
  57.8 1.9 %collective-permute-start.7 = (bf16[8,64,128]{2,1,0:T(8,128)(2,1)S(1)}, bf16[8,64,128]{2,1,0:T(8,128)(2,1)S(1)}, u32[]{:S(2)}, u32[]{:S(2)}) collective-permute-start(bf16[8,64,128]{2,1,0:T(8,128)(2,1)S(1)} %get-tuple-element.28), channel_id=1, source_target_pairs={{2,5},{3,4},{4,3},{5,2},{10,13},{11,12},{12,11},{13,10},{18,21},{1... | collective-permute-start | bytes 393224 | tf_op jit(solution)/shard_map/ppermute | solution.py:329
  59.7 2.8 %collective-permute-start = (bf16[8,64,128]{2,1,0:T(8,128)(2,1)S(1)}, bf16[8,64,128]{2,1,0:T(8,128)(2,1)S(1)}, u32[]{:S(2)}, u32[]{:S(2)}) collective-permute-start(bf16[8,64,128]{2,1,0:T(8,128)(2,1)S(1)} %get-tuple-element.17), channel_id=1, source_target_pairs={{2,4},{3,5},{4,2},{5,3},{10,12},{11,13},{12,10},{13,11},{18,20},{1... | collective-permute-start | bytes 393224 | tf_op jit(solution)/shard_map/ppermute | solution.py:329
  62.5 3.9 %collective-permute-start.1 = (bf16[8,64,128]{2,1,0:T(8,128)(2,1)S(1)}, bf16[8,64,128]{2,1,0:T(8,128)(2,1)S(1)}, u32[]{:S(2)}, u32[]{:S(2)}) collective-permute-start(bf16[8,64,128]{2,1,0:T(8,128)(2,1)S(1)} %get-tuple-element.18), channel_id=1, source_target_pairs={{2,5},{3,4},{4,3},{5,2},{10,13},{11,12},{12,11},{13,10},{18,21},{1... | collective-permute-start | bytes 393224 | tf_op jit(solution)/shard_map/ppermute | solution.py:329
  66.5 9.3 %collective-permute-done.4.same_ref = bf16[8,64,128]{2,1,0:T(8,128)(2,1)S(1)} collective-permute-done((bf16[8,64,128]{2,1,0:T(8,128)(2,1)S(1)}, bf16[8,64,128]{2,1,0:T(8,128)(2,1)S(1)}, u32[]{:S(2)}, u32[]{:S(2)}) %collective-permute-start.4) | collective-permute-done | bytes 131104 | tf_op jit(solution)/shard_map/ppermute | solution.py:329
  75.8 2.9 %collective-permute-start.2 = (bf16[8,64,128]{2,1,0:T(8,128)(2,1)S(1)}, bf16[8,64,128]{2,1,0:T(8,128)(2,1)S(1)}, u32[]{:S(2)}, u32[]{:S(2)}) collective-permute-start(bf16[8,64,128]{2,1,0:T(8,128)(2,1)S(1)} %get-tuple-element.23), channel_id=1, source_target_pairs={{2,4},{3,5},{4,2},{5,3},{10,12},{11,13},{12,10},{13,11},{18,20},{1... | collective-permute-start | bytes 393224 | tf_op jit(solution)/shard_map/ppermute | solution.py:329
  78.7 0.0 collective-permute-done.6.same_ref
  78.7 2.9 %collective-permute-start.3 = (bf16[8,64,128]{2,1,0:T(8,128)(2,1)S(1)}, bf16[8,64,128]{2,1,0:T(8,128)(2,1)S(1)}, u32[]{:S(2)}, u32[]{:S(2)}) collective-permute-start(bf16[8,64,128]{2,1,0:T(8,128)(2,1)S(1)} %get-tuple-element.24), channel_id=1, source_target_pairs={{2,5},{3,4},{4,3},{5,2},{10,13},{11,12},{12,11},{13,10},{18,21},{1... | collective-permute-start | bytes 393224 | tf_op jit(solution)/shard_map/ppermute | solution.py:329
  81.6 0.0 collective-permute-done.7.other_ref
  81.6 3.0 %collective-permute-start.5 = (bf16[8,64,128]{2,1,0:T(8,128)(2,1)S(1)}, bf16[8,64,128]{2,1,0:T(8,128)(2,1)S(1)}, u32[]{:S(2)}, u32[]{:S(2)}) collective-permute-start(bf16[8,64,128]{2,1,0:T(8,128)(2,1)S(1)} %get-tuple-element.26), channel_id=1, source_target_pairs={{2,5},{3,4},{4,3},{5,2},{10,13},{11,12},{12,11},{13,10},{18,21},{1... | collective-permute-start | bytes 393224 | tf_op jit(solution)/shard_map/ppermute | solution.py:329
  84.6 2.3 %most.1.most_ref = f32[8,512,512]{2,1,0:T(8,128)S(1)} custom-call(bf16[8,512,512]{2,1,0:T(8,128)(2,1)S(1)} %get-tuple-element.21.g_ref, bf16[512,512]{1,0:T(8,128)(2,1)S(1)} %get-tuple-element.22.l4_ref), custom_call_target="tpu_custom_call" | custom-call | flops 2147483648 | bytes 12582912 | tf_op jit(solution)/shard_map/most/pallas_call | solution.py:331
  86.9 1.8 %shard_map.28.refs_0_ = f32[64,64,512]{2,1,0:T(8,128)} custom-call(bf16[8,64,128]{2,1,0:T(8,128)(2,1)S(1)} %collective-permute-done.6.same_ref, bf16[8,64,128]{2,1,0:T(8,128)(2,1)S(1)} %collective-permute-done.7.other_ref, bf16[64,64]{1,0:T(8,128)(2,1)S(1)} %get-tuple-element.19.ct_ref, bf16[512,128]{1,0:T(8,128)(2,1)S(1)} %get-tuple-element.20.l4n_ref, ...), custom_call_target="tpu_custom_call" | custom-call | flops 134217728 | bytes 4194304 | tf_op jit(solution)/shard_map/pallas_call | solution.py:343
  88.7 6.5 %collective-permute-done.5.other_ref = bf16[8,64,128]{2,1,0:T(8,128)(2,1)S(1)} collective-permute-done((bf16[8,64,128]{2,1,0:T(8,128)(2,1)S(1)}, bf16[8,64,128]{2,1,0:T(8,128)(2,1)S(1)}, u32[]{:S(2)}, u32[]{:S(2)}) %collective-permute-start.5) | collective-permute-done | bytes 131104 | tf_op jit(solution)/shard_map/ppermute | solution.py:329
  95.2 1.8 %shard_map.29.refs_0_ = f32[64,64,512]{2,1,0:T(8,128)} custom-call(bf16[8,64,128]{2,1,0:T(8,128)(2,1)S(1)} %collective-permute-done.4.same_ref, bf16[8,64,128]{2,1,0:T(8,128)(2,1)S(1)} %collective-permute-done.5.other_ref, bf16[64,64]{1,0:T(8,128)(2,1)S(1)} %get-tuple-element.19.ct_ref, ...), custom_call_target="tpu_custom_call", output_to_operand_aliasing={{}: (5, {})} | custom-call | flops 134217728 | bytes 4194304 | tf_op jit(solution)/shard_map/pallas_call | solution.py:343
  97.0 0.0 collective-permute-done.2.same_ref
  97.0 0.0 collective-permute-done.3.other_ref
  97.0 1.8 %shard_map.30.refs_0_ = f32[64,64,512]{2,1,0:T(8,128)} custom-call(bf16[8,64,128]{2,1,0:T(8,128)(2,1)S(1)} %collective-permute-done.2.same_ref, bf16[8,64,128]{2,1,0:T(8,128)(2,1)S(1)} %collective-permute-done.3.other_ref, bf16[64,64]{1,0:T(8,128)(2,1)S(1)} %get-tuple-element.19.ct_ref, ...), custom_call_target="tpu_custom_call", output_to_operand_aliasing={{}: (5, {})} | custom-call | flops 134217728 | bytes 4194304 | tf_op jit(solution)/shard_map/pallas_call | solution.py:343
  98.8 0.0 collective-permute-done.same_ref
  98.8 0.0 collective-permute-done.1.other_ref
  98.8 1.8 %shard_map.31 = f32[64,64,512]{2,1,0:T(8,128)} custom-call(bf16[8,64,128]{2,1,0:T(8,128)(2,1)S(1)} %collective-permute-done.same_ref, bf16[8,64,128]{2,1,0:T(8,128)(2,1)S(1)} %collective-permute-done.1.other_ref, bf16[64,64]{1,0:T(8,128)(2,1)S(1)} %get-tuple-element.19.ct_ref, ...), custom_call_target="tpu_custom_call", output_to_operand_aliasing={{}: (5, {})} | custom-call | flops 134217728 | bytes 4194304 | tf_op jit(solution)/shard_map/pallas_call | solution.py:343
Async XLA Ops:
  52.5 23.2 %collective-permute-start.4 = (bf16[8,64,128]{2,1,0:T(8,128)(2,1)S(1)}, bf16[8,64,128]{2,1,0:T(8,128)(2,1)S(1)}, u32[]{:S(2)}, u32[]{:S(2)}) collective-permute-start(bf16[8,64,128]{2,1,0:T(8,128)(2,1)S(1)} %get-tuple-element.25), channel_id=1, source_target_pairs={{2,4},{3,5},{4,2},{5,3},{10,12},{11,13},{12,10},{13,11},{18,20},{1... | collective-permute-start | bytes 393224 | tf_op jit(solution)/shard_map/ppermute | solution.py:329
  55.3 23.4 %collective-permute-start.6 = (bf16[8,64,128]{2,1,0:T(8,128)(2,1)S(1)}, bf16[8,64,128]{2,1,0:T(8,128)(2,1)S(1)}, u32[]{:S(2)}, u32[]{:S(2)}) collective-permute-start(bf16[8,64,128]{2,1,0:T(8,128)(2,1)S(1)} %get-tuple-element.27), channel_id=1, source_target_pairs={{2,4},{3,5},{4,2},{5,3},{10,12},{11,13},{12,10},{13,11},{18,20},{1... | collective-permute-start | bytes 393224 | tf_op jit(solution)/shard_map/ppermute | solution.py:329
  57.8 23.8 %collective-permute-start.7 = (bf16[8,64,128]{2,1,0:T(8,128)(2,1)S(1)}, bf16[8,64,128]{2,1,0:T(8,128)(2,1)S(1)}, u32[]{:S(2)}, u32[]{:S(2)}) collective-permute-start(bf16[8,64,128]{2,1,0:T(8,128)(2,1)S(1)} %get-tuple-element.28), channel_id=1, source_target_pairs={{2,5},{3,4},{4,3},{5,2},{10,13},{11,12},{12,11},{13,10},{18,21},{1... | collective-permute-start | bytes 393224 | tf_op jit(solution)/shard_map/ppermute | solution.py:329
  59.7 39.1 %collective-permute-start = (bf16[8,64,128]{2,1,0:T(8,128)(2,1)S(1)}, bf16[8,64,128]{2,1,0:T(8,128)(2,1)S(1)}, u32[]{:S(2)}, u32[]{:S(2)}) collective-permute-start(bf16[8,64,128]{2,1,0:T(8,128)(2,1)S(1)} %get-tuple-element.17), channel_id=1, source_target_pairs={{2,4},{3,5},{4,2},{5,3},{10,12},{11,13},{12,10},{13,11},{18,20},{1... | collective-permute-start | bytes 393224 | tf_op jit(solution)/shard_map/ppermute | solution.py:329
  62.5 36.3 %collective-permute-start.1 = (bf16[8,64,128]{2,1,0:T(8,128)(2,1)S(1)}, bf16[8,64,128]{2,1,0:T(8,128)(2,1)S(1)}, u32[]{:S(2)}, u32[]{:S(2)}) collective-permute-start(bf16[8,64,128]{2,1,0:T(8,128)(2,1)S(1)} %get-tuple-element.18), channel_id=1, source_target_pairs={{2,5},{3,4},{4,3},{5,2},{10,13},{11,12},{12,11},{13,10},{18,21},{1... | collective-permute-start | bytes 393224 | tf_op jit(solution)/shard_map/ppermute | solution.py:329
  75.8 21.3 %collective-permute-start.2 = (bf16[8,64,128]{2,1,0:T(8,128)(2,1)S(1)}, bf16[8,64,128]{2,1,0:T(8,128)(2,1)S(1)}, u32[]{:S(2)}, u32[]{:S(2)}) collective-permute-start(bf16[8,64,128]{2,1,0:T(8,128)(2,1)S(1)} %get-tuple-element.23), channel_id=1, source_target_pairs={{2,4},{3,5},{4,2},{5,3},{10,12},{11,13},{12,10},{13,11},{18,20},{1... | collective-permute-start | bytes 393224 | tf_op jit(solution)/shard_map/ppermute | solution.py:329
  78.7 18.3 %collective-permute-start.3 = (bf16[8,64,128]{2,1,0:T(8,128)(2,1)S(1)}, bf16[8,64,128]{2,1,0:T(8,128)(2,1)S(1)}, u32[]{:S(2)}, u32[]{:S(2)}) collective-permute-start(bf16[8,64,128]{2,1,0:T(8,128)(2,1)S(1)} %get-tuple-element.24), channel_id=1, source_target_pairs={{2,5},{3,4},{4,3},{5,2},{10,13},{11,12},{12,11},{13,10},{18,21},{1... | collective-permute-start | bytes 393224 | tf_op jit(solution)/shard_map/ppermute | solution.py:329
  81.6 13.6 %collective-permute-start.5 = (bf16[8,64,128]{2,1,0:T(8,128)(2,1)S(1)}, bf16[8,64,128]{2,1,0:T(8,128)(2,1)S(1)}, u32[]{:S(2)}, u32[]{:S(2)}) collective-permute-start(bf16[8,64,128]{2,1,0:T(8,128)(2,1)S(1)} %get-tuple-element.26), channel_id=1, source_target_pairs={{2,5},{3,4},{4,3},{5,2},{10,13},{11,12},{12,11},{13,10},{18,21},{1... | collective-permute-start | bytes 393224 | tf_op jit(solution)/shard_map/ppermute | solution.py:329

commit v5 on v4

--- a/solution.py
+++ b/solution.py
@@ -32,7 +32,6 @@
     core = me % 2
 
     load_c = pltpu.make_async_copy(c_hbm, c_vm, c_sem)
-    load_c.start()
 
     def load_row(p):
         return pltpu.make_async_copy(a_hbm.at[p], a_vm.at[p], a_sem.at[p])
@@ -41,15 +40,15 @@
         half = pl.ds(32 * h, 32)
         return pltpu.make_async_copy(a_hbm.at[0, half], a_vm.at[0, half], a_sem.at[ROWS * h])
 
-    for h in range(2):
-        load_half(h).start()
+    load_half(0).start()
+    load_c.start()
+    load_half(1).start()
 
     barrier = pltpu.get_barrier_semaphore()
     for k in range(1, DEV):
         pl.semaphore_signal(barrier, inc=1, device_id={"dev": (me + k) % DEV}, device_id_type=pl.DeviceIdType.MESH)
 
     load_c.wait()
-    load_row(1).start()
     c = c_vm[...]
     nt = (((1,), (1,)), ((), ()))
     wide = (8 * N, 8 * N)
@@ -80,14 +79,32 @@
             device_id_type=pl.DeviceIdType.MESH,
         )
 
+    def half(h, dest, src):
+        part = pl.ds(32 * h, 32)
+        return pltpu.make_async_remote_copy(
+            src_ref=send.at[dest, 0, part],
+            dst_ref=recv.at[src, 0, part],
+            send_sem=send_sem.at[dest, ROWS * h],
+            recv_sem=recv_sem.at[src, ROWS * h],
+            device_id={"dev": dest},
+            device_id_type=pl.DeviceIdType.MESH,
+        )
+
+    def copies(rows, dest, src):
+        if rows == EARLY[0]:
+            return [half(h, dest, src) for h in range(2)]
+        return [group(rows, dest, src)]
+
     def start(rows, to):
         for k in range(2):
-            group(rows, 2 * to + k, me).start()
+            for copy in copies(rows, 2 * to + k, me):
+                copy.start()
 
     def sent(groups, to):
         for rows in groups:
             for k in range(2):
-                group(rows, 2 * to + k, me).wait_send()
+                for copy in copies(rows, 2 * to + k, me):
+                    copy.wait_send()
 
     low = iota((32, 8, 128), 2) < N
 
@@ -114,11 +131,11 @@
 
         pieces(p, h, l_vm[...], 32, put)
 
-    def chip_piece(p, to, lhs):
+    def chip_piece(p, halves, to, lhs):
         def put(dest, q, columns, value):
             send[2 * to + dest, p, q, columns] = value
 
-        for h in range(2):
+        for h in halves:
             pieces(p, h, lhs, 8, put)
 
     is_edge = jnp.logical_or(chip == 0, chip == 3)
@@ -134,13 +151,17 @@
     l_vm[:128, :] = kron_rows(16 * first_chip, 16)
     for h in range(2):
         load_half(h).wait()
-    load_row(2).start()
-    chip_piece(0, first_chip, l_vm[:128, :])
-    pl.semaphore_wait(barrier, DEV - 1)
-    start(EARLY[0], first_chip)
+        if h == 1:
+            for later in (1, 2):
+                load_row(later).start()
+        chip_piece(0, (h,), first_chip, l_vm[:128, :])
+        if h == 0:
+            pl.semaphore_wait(barrier, DEV - 1)
+        for k in range(2):
+            half(h, 2 * first_chip + k, me).start()
     load_row(1).wait()
     load_row(3).start()
-    chip_piece(1, first_chip, l_vm[:128, :])
+    chip_piece(1, range(2), first_chip, l_vm[:128, :])
     start(EARLY[1], first_chip)
 
     l_vm[...] = kron_rows(0, N)
@@ -148,8 +169,9 @@
     fourth_chip = jnp.where(is_edge, last, near)
     for p in range(2):
         for to in (second_chip, fourth_chip, chip):
-            chip_piece(p, to, l_vm[pl.ds(pl.multiple_of(128 * to, 128), 128), :])
-        group(EARLY[p], partner, me).start()
+            chip_piece(p, range(2), to, l_vm[pl.ds(pl.multiple_of(128 * to, 128), 128), :])
+        for copy in copies(EARLY[p], partner, me):
+            copy.start()
 
         @pl.when(jnp.logical_not(is_edge))
         def _():
@@ -216,7 +238,8 @@
     def take(groups, sources):
         for rows in groups:
             for src in sources:
-                group(rows, src, src).wait_recv()
+                for copy in copies(rows, src, src):
+                    copy.wait_recv()
             if sum(rows) % 2 == 0:
                 begin = rows[0] // 2 * 2
 
@@ -237,7 +260,8 @@
     take(EARLY, [2 * beside, 2 * beside + 1])
 
     for rows in EARLY:
-        group(rows, partner, me).wait_send()
+        for copy in copies(rows, partner, me):
+            copy.wait_send()
     sent(EARLY, beside)
 
     @pl.when(is_edge)
@@ -314,8 +338,8 @@
                 pltpu.VMEM((DEV, ROWS, N, COLS), BF16),
                 pltpu.SemaphoreType.DMA((ROWS + 1,)),
                 pltpu.SemaphoreType.DMA,
-                pltpu.SemaphoreType.DMA((DEV, ROWS)),
-                pltpu.SemaphoreType.DMA((DEV, ROWS)),
+                pltpu.SemaphoreType.DMA((DEV, ROWS + 1)),
+                pltpu.SemaphoreType.DMA((DEV, ROWS + 1)),
             ],
             compiler_params=pltpu.CompilerParams(collective_id=0, has_side_effects=True, vmem_limit_bytes=40 * 2**20),
             name="exchange",

time: 101 us -> 101 us (level)
  the two profiles are of different devices: /device:TPU:13 before, /device:TPU:17 now
where the time goes in v5:
time: 101 us
  Pallas kernels  61.8 us (61%)
  starting transfers between devices  21.1 us (21%)
  waiting for transfers between devices  17.5 us (17%)
    pallas_call x1, Pallas kernels, local_transform(): pl.pallas_call(exchange_kernel, out_shape=outs, in_specs=[anywhere, anywh...  52.4 us
    ppermute x8, starting transfers between devices, local_transform(): pair.append(lax.ppermute(near[side * CHUNKS + chunk], 'dev', perm))  21.1 us
    ppermute x8, waiting for transfers between devices, local_transform(): pair.append(lax.ppermute(near[side * CHUNKS + chunk], 'dev', perm))  17.5 us
    pallas_call x4, Pallas kernels, local_transform(): pl.pallas_call(functools.partial(chunk_kernel, chunk), out_shape=sds((N,...  7.13 us
    pallas_call x1, Pallas kernels, local_transform(): pl.pallas_call(most_kernel, out_shape=sds((8, 8 * N, COLS), F32), in_spec...  2.34 us
  transfers between devices with their start and end apart: 8, of which 3 were waited for; matrix products, arithmetic and copies ran while one was open for 0% of the time, Pallas kernels for 8%

profile of v5, /device:TPU:17, one launch (start us, length us, event | category | flops | bytes accessed | tf_op | source)
XLA Modules:
  0.0 100.5 jit_solution(10637634158652778010)
XLA Ops:
  0.0 52.4 %exchange.1 = (bf16[8,512,512]{2,1,0:T(8,128)(2,1)S(1)}, bf16[512,512]{1,0:T(8,128)(2,1)S(1)}, bf16[512,128]{1,0:T(8,128)(2,1)S(1)}, bf16[64,64]{1,0:T(8,128)(2,...) custom-call(bf16[8,64,64,64]{3,2,1,0:T(8,128)(2,1)} %a_hbm.1, ...), custom_call_target="tpu_custom_call" | custom-call | tf_op jit(solution)/shard_map/exchange/pallas_call | solution.py:326
  52.4 2.3 %collective-permute-start.4 = (bf16[8,64,128]{2,1,0:T(8,128)(2,1)S(1)}, bf16[8,64,128]{2,1,0:T(8,128)(2,1)S(1)}, u32[]{:S(2)}, u32[]{:S(2)}) collective-permute-start(bf16[8,64,128]{2,1,0:T(8,128)(2,1)S(1)} %get-tuple-element.25), channel_id=1, source_target_pairs={{2,4},{3,5},{4,2},{5,3},{10,12},{11,13},{12,10},{13,11},{18,20},{1... | collective-permute-start | bytes 393224 | tf_op jit(solution)/shard_map/ppermute | solution.py:353
  54.7 2.9 %collective-permute-start.6 = (bf16[8,64,128]{2,1,0:T(8,128)(2,1)S(1)}, bf16[8,64,128]{2,1,0:T(8,128)(2,1)S(1)}, u32[]{:S(2)}, u32[]{:S(2)}) collective-permute-start(bf16[8,64,128]{2,1,0:T(8,128)(2,1)S(1)} %get-tuple-element.27), channel_id=1, source_target_pairs={{2,4},{3,5},{4,2},{5,3},{10,12},{11,13},{12,10},{13,11},{18,20},{1... | collective-permute-start | bytes 393224 | tf_op jit(solution)/shard_map/ppermute | solution.py:353
  57.7 1.9 %collective-permute-start.7 = (bf16[8,64,128]{2,1,0:T(8,128)(2,1)S(1)}, bf16[8,64,128]{2,1,0:T(8,128)(2,1)S(1)}, u32[]{:S(2)}, u32[]{:S(2)}) collective-permute-start(bf16[8,64,128]{2,1,0:T(8,128)(2,1)S(1)} %get-tuple-element.28), channel_id=1, source_target_pairs={{2,5},{3,4},{4,3},{5,2},{10,13},{11,12},{12,11},{13,10},{18,21},{1... | collective-permute-start | bytes 393224 | tf_op jit(solution)/shard_map/ppermute | solution.py:353
  59.6 2.3 %collective-permute-start = (bf16[8,64,128]{2,1,0:T(8,128)(2,1)S(1)}, bf16[8,64,128]{2,1,0:T(8,128)(2,1)S(1)}, u32[]{:S(2)}, u32[]{:S(2)}) collective-permute-start(bf16[8,64,128]{2,1,0:T(8,128)(2,1)S(1)} %get-tuple-element.17), channel_id=1, source_target_pairs={{2,4},{3,5},{4,2},{5,3},{10,12},{11,13},{12,10},{13,11},{18,20},{1... | collective-permute-start | bytes 393224 | tf_op jit(solution)/shard_map/ppermute | solution.py:353
  62.0 3.9 %collective-permute-start.1 = (bf16[8,64,128]{2,1,0:T(8,128)(2,1)S(1)}, bf16[8,64,128]{2,1,0:T(8,128)(2,1)S(1)}, u32[]{:S(2)}, u32[]{:S(2)}) collective-permute-start(bf16[8,64,128]{2,1,0:T(8,128)(2,1)S(1)} %get-tuple-element.18), channel_id=1, source_target_pairs={{2,5},{3,4},{4,3},{5,2},{10,13},{11,12},{12,11},{13,10},{18,21},{1... | collective-permute-start | bytes 393224 | tf_op jit(solution)/shard_map/ppermute | solution.py:353
  65.9 9.8 %collective-permute-done.4.same_ref = bf16[8,64,128]{2,1,0:T(8,128)(2,1)S(1)} collective-permute-done((bf16[8,64,128]{2,1,0:T(8,128)(2,1)S(1)}, bf16[8,64,128]{2,1,0:T(8,128)(2,1)S(1)}, u32[]{:S(2)}, u32[]{:S(2)}) %collective-permute-start.4) | collective-permute-done | bytes 131104 | tf_op jit(solution)/shard_map/ppermute | solution.py:353
  75.7 2.1 %collective-permute-start.2 = (bf16[8,64,128]{2,1,0:T(8,128)(2,1)S(1)}, bf16[8,64,128]{2,1,0:T(8,128)(2,1)S(1)}, u32[]{:S(2)}, u32[]{:S(2)}) collective-permute-start(bf16[8,64,128]{2,1,0:T(8,128)(2,1)S(1)} %get-tuple-element.23), channel_id=1, source_target_pairs={{2,4},{3,5},{4,2},{5,3},{10,12},{11,13},{12,10},{13,11},{18,20},{1... | collective-permute-start | bytes 393224 | tf_op jit(solution)/shard_map/ppermute | solution.py:353
  77.7 0.6 collective-permute-done.6.same_ref
  78.3 3.0 %collective-permute-start.3 = (bf16[8,64,128]{2,1,0:T(8,128)(2,1)S(1)}, bf16[8,64,128]{2,1,0:T(8,128)(2,1)S(1)}, u32[]{:S(2)}, u32[]{:S(2)}) collective-permute-start(bf16[8,64,128]{2,1,0:T(8,128)(2,1)S(1)} %get-tuple-element.24), channel_id=1, source_target_pairs={{2,5},{3,4},{4,3},{5,2},{10,13},{11,12},{12,11},{13,10},{18,21},{1... | collective-permute-start | bytes 393224 | tf_op jit(solution)/shard_map/ppermute | solution.py:353
  81.3 0.0 collective-permute-done.7.other_ref
  81.3 2.5 %collective-permute-start.5 = (bf16[8,64,128]{2,1,0:T(8,128)(2,1)S(1)}, bf16[8,64,128]{2,1,0:T(8,128)(2,1)S(1)}, u32[]{:S(2)}, u32[]{:S(2)}) collective-permute-start(bf16[8,64,128]{2,1,0:T(8,128)(2,1)S(1)} %get-tuple-element.26), channel_id=1, source_target_pairs={{2,5},{3,4},{4,3},{5,2},{10,13},{11,12},{12,11},{13,10},{18,21},{1... | collective-permute-start | bytes 393224 | tf_op jit(solution)/shard_map/ppermute | solution.py:353
  83.9 2.3 %most.1.most_ref = f32[8,512,512]{2,1,0:T(8,128)S(1)} custom-call(bf16[8,512,512]{2,1,0:T(8,128)(2,1)S(1)} %get-tuple-element.21.g_ref, bf16[512,512]{1,0:T(8,128)(2,1)S(1)} %get-tuple-element.22.l4_ref), custom_call_target="tpu_custom_call" | custom-call | flops 2147483648 | bytes 12582912 | tf_op jit(solution)/shard_map/most/pallas_call | solution.py:355
  86.2 1.8 %shard_map.28.refs_0_ = f32[64,64,512]{2,1,0:T(8,128)} custom-call(bf16[8,64,128]{2,1,0:T(8,128)(2,1)S(1)} %collective-permute-done.6.same_ref, bf16[8,64,128]{2,1,0:T(8,128)(2,1)S(1)} %collective-permute-done.7.other_ref, bf16[64,64]{1,0:T(8,128)(2,1)S(1)} %get-tuple-element.19.ct_ref, bf16[512,128]{1,0:T(8,128)(2,1)S(1)} %get-tuple-element.20.l4n_ref, ...), custom_call_target="tpu_custom_call" | custom-call | flops 134217728 | bytes 4194304 | tf_op jit(solution)/shard_map/pallas_call | solution.py:367
  88.0 7.1 %collective-permute-done.5.other_ref = bf16[8,64,128]{2,1,0:T(8,128)(2,1)S(1)} collective-permute-done((bf16[8,64,128]{2,1,0:T(8,128)(2,1)S(1)}, bf16[8,64,128]{2,1,0:T(8,128)(2,1)S(1)}, u32[]{:S(2)}, u32[]{:S(2)}) %collective-permute-start.5) | collective-permute-done | bytes 131104 | tf_op jit(solution)/shard_map/ppermute | solution.py:353
  95.1 1.8 %shard_map.29.refs_0_ = f32[64,64,512]{2,1,0:T(8,128)} custom-call(bf16[8,64,128]{2,1,0:T(8,128)(2,1)S(1)} %collective-permute-done.4.same_ref, bf16[8,64,128]{2,1,0:T(8,128)(2,1)S(1)} %collective-permute-done.5.other_ref, bf16[64,64]{1,0:T(8,128)(2,1)S(1)} %get-tuple-element.19.ct_ref, ...), custom_call_target="tpu_custom_call", output_to_operand_aliasing={{}: (5, {})} | custom-call | flops 134217728 | bytes 4194304 | tf_op jit(solution)/shard_map/pallas_call | solution.py:367
  96.9 0.0 collective-permute-done.2.same_ref
  96.9 0.0 collective-permute-done.3.other_ref
  96.9 1.8 %shard_map.30.refs_0_ = f32[64,64,512]{2,1,0:T(8,128)} custom-call(bf16[8,64,128]{2,1,0:T(8,128)(2,1)S(1)} %collective-permute-done.2.same_ref, bf16[8,64,128]{2,1,0:T(8,128)(2,1)S(1)} %collective-permute-done.3.other_ref, bf16[64,64]{1,0:T(8,128)(2,1)S(1)} %get-tuple-element.19.ct_ref, ...), custom_call_target="tpu_custom_call", output_to_operand_aliasing={{}: (5, {})} | custom-call | flops 134217728 | bytes 4194304 | tf_op jit(solution)/shard_map/pallas_call | solution.py:367
  98.7 0.0 collective-permute-done.same_ref
  98.7 0.0 collective-permute-done.1.other_ref
  98.8 1.8 %shard_map.31 = f32[64,64,512]{2,1,0:T(8,128)} custom-call(bf16[8,64,128]{2,1,0:T(8,128)(2,1)S(1)} %collective-permute-done.same_ref, bf16[8,64,128]{2,1,0:T(8,128)(2,1)S(1)} %collective-permute-done.1.other_ref, bf16[64,64]{1,0:T(8,128)(2,1)S(1)} %get-tuple-element.19.ct_ref, ...), custom_call_target="tpu_custom_call", output_to_operand_aliasing={{}: (5, {})} | custom-call | flops 134217728 | bytes 4194304 | tf_op jit(solution)/shard_map/pallas_call | solution.py:367
Async XLA Ops:
  52.4 23.3 %collective-permute-start.4 = (bf16[8,64,128]{2,1,0:T(8,128)(2,1)S(1)}, bf16[8,64,128]{2,1,0:T(8,128)(2,1)S(1)}, u32[]{:S(2)}, u32[]{:S(2)}) collective-permute-start(bf16[8,64,128]{2,1,0:T(8,128)(2,1)S(1)} %get-tuple-element.25), channel_id=1, source_target_pairs={{2,4},{3,5},{4,2},{5,3},{10,12},{11,13},{12,10},{13,11},{18,20},{1... | collective-permute-start | bytes 393224 | tf_op jit(solution)/shard_map/ppermute | solution.py:353
  54.7 23.5 %collective-permute-start.6 = (bf16[8,64,128]{2,1,0:T(8,128)(2,1)S(1)}, bf16[8,64,128]{2,1,0:T(8,128)(2,1)S(1)}, u32[]{:S(2)}, u32[]{:S(2)}) collective-permute-start(bf16[8,64,128]{2,1,0:T(8,128)(2,1)S(1)} %get-tuple-element.27), channel_id=1, source_target_pairs={{2,4},{3,5},{4,2},{5,3},{10,12},{11,13},{12,10},{13,11},{18,20},{1... | collective-permute-start | bytes 393224 | tf_op jit(solution)/shard_map/ppermute | solution.py:353
  57.7 23.6 %collective-permute-start.7 = (bf16[8,64,128]{2,1,0:T(8,128)(2,1)S(1)}, bf16[8,64,128]{2,1,0:T(8,128)(2,1)S(1)}, u32[]{:S(2)}, u32[]{:S(2)}) collective-permute-start(bf16[8,64,128]{2,1,0:T(8,128)(2,1)S(1)} %get-tuple-element.28), channel_id=1, source_target_pairs={{2,5},{3,4},{4,3},{5,2},{10,13},{11,12},{12,11},{13,10},{18,21},{1... | collective-permute-start | bytes 393224 | tf_op jit(solution)/shard_map/ppermute | solution.py:353
  59.6 39.1 %collective-permute-start = (bf16[8,64,128]{2,1,0:T(8,128)(2,1)S(1)}, bf16[8,64,128]{2,1,0:T(8,128)(2,1)S(1)}, u32[]{:S(2)}, u32[]{:S(2)}) collective-permute-start(bf16[8,64,128]{2,1,0:T(8,128)(2,1)S(1)} %get-tuple-element.17), channel_id=1, source_target_pairs={{2,4},{3,5},{4,2},{5,3},{10,12},{11,13},{12,10},{13,11},{18,20},{1... | collective-permute-start | bytes 393224 | tf_op jit(solution)/shard_map/ppermute | solution.py:353
  62.0 36.8 %collective-permute-start.1 = (bf16[8,64,128]{2,1,0:T(8,128)(2,1)S(1)}, bf16[8,64,128]{2,1,0:T(8,128)(2,1)S(1)}, u32[]{:S(2)}, u32[]{:S(2)}) collective-permute-start(bf16[8,64,128]{2,1,0:T(8,128)(2,1)S(1)} %get-tuple-element.18), channel_id=1, source_target_pairs={{2,5},{3,4},{4,3},{5,2},{10,13},{11,12},{12,11},{13,10},{18,21},{1... | collective-permute-start | bytes 393224 | tf_op jit(solution)/shard_map/ppermute | solution.py:353
  75.7 21.3 %collective-permute-start.2 = (bf16[8,64,128]{2,1,0:T(8,128)(2,1)S(1)}, bf16[8,64,128]{2,1,0:T(8,128)(2,1)S(1)}, u32[]{:S(2)}, u32[]{:S(2)}) collective-permute-start(bf16[8,64,128]{2,1,0:T(8,128)(2,1)S(1)} %get-tuple-element.23), channel_id=1, source_target_pairs={{2,4},{3,5},{4,2},{5,3},{10,12},{11,13},{12,10},{13,11},{18,20},{1... | collective-permute-start | bytes 393224 | tf_op jit(solution)/shard_map/ppermute | solution.py:353
  78.3 18.7 %collective-permute-start.3 = (bf16[8,64,128]{2,1,0:T(8,128)(2,1)S(1)}, bf16[8,64,128]{2,1,0:T(8,128)(2,1)S(1)}, u32[]{:S(2)}, u32[]{:S(2)}) collective-permute-start(bf16[8,64,128]{2,1,0:T(8,128)(2,1)S(1)} %get-tuple-element.24), channel_id=1, source_target_pairs={{2,5},{3,4},{4,3},{5,2},{10,13},{11,12},{12,11},{13,10},{18,21},{1... | collective-permute-start | bytes 393224 | tf_op jit(solution)/shard_map/ppermute | solution.py:353
  81.3 13.8 %collective-permute-start.5 = (bf16[8,64,128]{2,1,0:T(8,128)(2,1)S(1)}, bf16[8,64,128]{2,1,0:T(8,128)(2,1)S(1)}, u32[]{:S(2)}, u32[]{:S(2)}) collective-permute-start(bf16[8,64,128]{2,1,0:T(8,128)(2,1)S(1)} %get-tuple-element.26), channel_id=1, source_target_pairs={{2,5},{3,4},{4,3},{5,2},{10,13},{11,12},{12,11},{13,10},{18,21},{1... | collective-permute-start | bytes 393224 | tf_op jit(solution)/shard_map/ppermute | solution.py:353
